TPU v7x, 32 devices: a whole 2x2x4 slice. The times are simulated.
32 devices in a mesh: grp: 8 (over z, core), blk: 4 (over y, x).
Axes of the slice: x: 2, y: 2, z: 4, core: 2. Of those that a mesh axis runs over, the one named last changes fastest.
Arguments:
- patches: float32 [256, 32, 1024], P(('grp', 'blk')), may hold values from -6 to 6
- counts: int32 [32], P(('grp', 'blk')), may hold values from 1 to 8
- moves: int32 [32, 4], P(('grp', 'blk')), may hold values from 0 to 3, as said below
- tags: int32 [8, 32], P('grp'), may hold values from 0 to 3
Outputs:
- fine: bfloat16 [256, 64, 4096], P(('grp', 'blk'))
Inputs may be any that keep to these rules, and one draw needn't show every extreme that they name: `moves`: each device holds between 1 and 8 live patches before and after every diffusion step, and hands on fewer patches than it holds at that step; in every draw some device hands on exactly 3 patches in some step.
All inputs are finite; a program needn't handle non-finite values.
Results may differ from a plain program's by a relative error of at most 0.001.
Values sent between devices are 32-bit elements; how exact they have to be, the bound alone decides.
No kernel may reach another device: no remote copies, remote signals or barrier semaphores. Data moves between devices by JAX's collectives and lax.ppermute only.
A program may use at most 128 MiB of HBM per device.

v0:
```python
import functools
import itertools

import jax
import jax.numpy as jnp
import numpy as np
from jax import lax
from jax.experimental import pallas as pl
from jax.experimental.pallas import tpu as pltpu
from jax.sharding import PartitionSpec as P


LANES = 128
SUBLANES = 8
CHOICES = (
    (4, 3, 3), (5, 4, 4), (3, 2, 2), (2, 4, 2), (2, 2, 2), (3, 5, 3), (3, 3, 3), (5, 2, 2), (4, 2, 2),
    (2, 3, 2), (2, 2, 3), (4, 1, 1), (1, 3, 1), (1, 1, 2), (3, 1, 1), (5, 1, 1), (1, 2, 1), (2, 2, 4),
    (6, 1, 1), (2, 1, 1), (2, 5, 2), (1, 1, 3), (1, 4, 1), (3, 4, 1), (3, 3, 1), (5, 3, 3), (1, 1, 1),
    (3, 2, 1), (1, 5, 1), (2, 2, 1), (2, 3, 1), (3, 1, 2), (4, 3, 1), (2, 1, 2), (4, 2, 1), (1, 2, 2),
)


def refine_table(edge, ghosts):
    finer = np.arange(2 * edge)[:, None]
    coarse = np.arange(edge + 2 * ghosts)[None, :]
    home = finer // 2 + ghosts
    side = home + 2 * (finer % 2) - 1
    return 0.75 * (coarse == home) + 0.25 * (coarse == side)


def window_table(edge):
    inner = LANES // edge - 2
    along_y = refine_table(inner, 1)
    along_z = refine_table(edge, 0)
    table = np.kron(along_y, along_z).T
    return jnp.asarray(np.concatenate([table, table], 0), jnp.bfloat16)


def refine_kernel(plan_ref, tag_ref, held_ref, work_ref, ends_ref, before_ref, table_ref, out_ref, rows_ref, split_ref):
    capacity = work_ref.shape[0]
    fine = out_ref.shape[1]
    edge, plane = (fine // 2, out_ref.shape[2] // 4)
    across = plane // LANES
    slot = pl.program_id(0)
    live = plan_ref[2, 0]

    @pl.when(slot >= live)
    def _():
        out_ref[...] = jnp.zeros_like(out_ref)

    @pl.when(slot < live)
    def _():
        factor = 1.0 + 0.5 * tag_ref[0, plan_ref[2, 1] + slot].astype(jnp.float32)

        def part(j, tiles, rows):
            j = jnp.clip(j, 0, capacity - 1)
            return jnp.where(plan_ref[0, j] == 0, held_ref[j, tiles, rows], work_ref[j, tiles, rows])

        def flat(tiles):
            tiles = tiles.reshape(-1, across, tiles.shape[-2], LANES)
            return jnp.concatenate([tiles[:, u].reshape(-1, LANES) for u in range(across)], axis=1)

        middle = flat(part(slot, slice(None), slice(None)))
        before = part(slot - 1, slice(edge // SUBLANES * across - across, None), slice(SUBLANES - 1, None))
        after = part(slot + 1, slice(0, across), slice(0, 1))
        lower = jnp.where(plan_ref[2, 4] == 0, ends_ref[0], before_ref[...])
        before = jnp.where(slot == 0, lower[:, None, :], before)
        after = jnp.where(slot == live - 1, ends_ref[1][:, None, :], after)
        before, after = flat(before), flat(after)
        place = lax.broadcasted_iota(jnp.int32, middle.shape, 0)
        below = jnp.where(place == 0, before, pltpu.roll(middle, 1, 0))
        above = jnp.where(place == edge - 1, after, pltpu.roll(middle, edge - 1, 0))
        home = middle * (0.75 * factor)
        even = home + below * (0.25 * factor)
        odd = home + above * (0.25 * factor)
        for u in range(plane // LANES):
            cut = slice(u * LANES, (u + 1) * LANES)
            rows_ref[u, pl.ds(0, edge, 2), :] = even[:, cut]
            rows_ref[u, pl.ds(1, edge, 2), :] = odd[:, cut]
        rows = jnp.concatenate([rows_ref[u] for u in range(plane // LANES)], axis=1)
        lane = lax.broadcasted_iota(jnp.int32, rows.shape, 1)
        later = jnp.where(lane < edge, 0.0, pltpu.roll(rows, edge, 1))
        sooner = jnp.where(lane >= plane - edge, 0.0, pltpu.roll(rows, plane - edge, 1))
        for side, moved in enumerate((later, sooner)):
            high = moved.astype(jnp.bfloat16)
            low = (moved - high.astype(jnp.float32)).astype(jnp.bfloat16)
            for u in range(plane // LANES):
                cut = slice(u * LANES, (u + 1) * LANES)
                split_ref[2 * u + side, :, :LANES] = high[:, cut]
                split_ref[2 * u + side, :, LANES:] = low[:, cut]
        windows, fine, depth = split_ref.shape
        width = table_ref.shape[1]
        table = table_ref[...]
        group = 4
        for g in range(0, windows, group):
            left = split_ref[g : g + group].reshape(group * fine, depth)
            product = jnp.dot(left, table, preferred_element_type=jnp.float32)
            for i in range(group):
                out_ref[0, :, (g + i) * width : (g + i + 1) * width] = product[i * fine : (i + 1) * fine].astype(jnp.bfloat16)


def refine(held, work, plan, tags, ends, before, edge):
    capacity, parts = work.shape[:2]
    plane = parts * SUBLANES * LANES // edge
    table = window_table(edge)
    windows = 2 * plane // LANES
    whole = lambda x: pl.BlockSpec(x.shape, lambda i, *_: (0,) * x.ndim)
    operands = (held, work, ends, before, table)
    return pl.pallas_call(
        refine_kernel,
        out_shape=jax.ShapeDtypeStruct((capacity, 2 * edge, 4 * plane), jnp.bfloat16),
        grid_spec=pltpu.PrefetchScalarGridSpec(
            num_scalar_prefetch=2,
            grid=(capacity,),
            in_specs=[whole(x) for x in operands],
            out_specs=pl.BlockSpec((1, 2 * edge, 4 * plane), lambda i, *_: (i, 0, 0)),
            scratch_shapes=[
                pltpu.VMEM((plane // LANES, 2 * edge, LANES), jnp.float32),
                pltpu.VMEM((windows, 2 * edge, 2 * LANES), jnp.bfloat16),
            ],
        ),
        compiler_params=pltpu.CompilerParams(vmem_limit_bytes=16 << 20),
        name="refine",
    )(plan, tags, *operands)


def swap(block, axis, bit):
    return lax.ppermute(block, axis, [(i, i ^ bit) for i in range(lax.axis_size(axis))])


def all_of(rows, axis):
    count, bit = (lax.axis_size(axis), 1)
    while bit < count:
        other = swap(rows, axis, bit)
        rows = jnp.concatenate([rows, other], 0)
        bit *= 2
    return rows


def forward(block, axis, distance):
    count = lax.axis_size(axis)
    return lax.ppermute(block, axis, [(i, (i + distance) % count) for i in range(count)])


def capacity_choices(distances, capacity):
    most = capacity - 1
    if distances == 3:
        choices = set(CHOICES)
    else:
        choices = {(u,) * distances for u in (1, 2, 3, 4)}
    choices = {tuple(min(c, most) for c in choice) for choice in choices} | {(most,) * distances}
    load = lambda c: (max(a + b for a, b in itertools.combinations(c + (0, 0), 2)), sum(c), c)
    return sorted(choices, key=load)


def tiled(patches):
    capacity, edge, plane = patches.shape
    cut = patches.reshape(capacity, edge // SUBLANES, SUBLANES, plane // LANES, LANES)
    return cut.transpose(0, 1, 3, 2, 4).reshape(capacity, -1, SUBLANES, LANES)


def last_plane(patches_ref, slot):
    return patches_ref.at[slot, pl.ds(patches_ref.shape[1] - SUBLANES, SUBLANES), SUBLANES - 1]


def first_plane(patches_ref, slot):
    return patches_ref.at[slot, pl.ds(0, SUBLANES), 0]


def plan_kernel(given_ref, plan_ref, pick_ref, *, choices, capacity, steps):
    devices = given_ref.shape[0]
    count = devices * max(1, SUBLANES // devices)
    shape = (count, LANES)
    wide = lambda column: jnp.broadcast_to(column, shape)
    behind = lambda x, k: pltpu.roll(x, k % count, 0) if k % count else x
    lane = lax.broadcasted_iota(jnp.int32, shape, 1)
    row = lax.broadcasted_iota(jnp.int32, shape, 0)
    given = given_ref[...]
    mine = given[0:1, steps + 1 : steps + 2]
    rows = jnp.zeros(shape, jnp.int32)
    for f in range(devices):
        ahead = given[f : f + 1, steps + 1 : steps + 2] - mine
        here = row % devices == jnp.where(ahead < 0, ahead + devices, ahead)
        rows = jnp.where(here, wide(given[f : f + 1]), rows)

    def trace(rows):
        starts, live = [], wide(rows[:, 0:1])
        for step in range(steps):
            sent = wide(rows[:, step + 1 : step + 2])
            starts.append(live - sent)
            live = starts[-1] + behind(sent, 1)
        back, place = jnp.zeros(shape, jnp.int32), lane
        for step in reversed(range(steps)):
            here, there = starts[step], behind(starts[step], 1)
            for k in range(1, steps - step):
                here = jnp.where(back == k, behind(starts[step], k), here)
                there = jnp.where(back == k, behind(starts[step], k + 1), there)
            came = place >= here
            place = jnp.where(came, place - here + there, place)
            back = jnp.where(came, back + 1, back)
        for _ in range(steps // devices):
            back = jnp.where(back >= devices, back - devices, back)
        return live, back, place

    def at_top(live, values):
        picked = jnp.where(lane == live - 1, values, 0).astype(jnp.float32)
        return wide(jnp.sum(picked, axis=1, keepdims=True)).astype(jnp.int32)

    live, back, place = trace(rows)
    start_flag = (wide(mine) == 0).astype(jnp.int32)
    top_back = behind(at_top(live, back), 1)
    top_place = jnp.clip(behind(at_top(live, place), 1), 0, capacity - 1)
    top_from = jnp.where(top_back + 1 >= devices, 0, top_back + 1)

    filled = lane < live
    source = jnp.where(filled, back, -1)
    rank = jnp.zeros(shape, jnp.int32)
    for j in range(capacity):
        rank = jnp.where((wide(source[:, j : j + 1]) == source) & (lane > j), rank + 1, rank)
    code = jnp.where(source == row, rank, -1)
    sent = jnp.zeros(shape, jnp.int32)
    for j in range(capacity):
        sent = jnp.where(wide(code[:, j : j + 1]) == lane, wide(place[:, j : j + 1]), sent)
    fits = None
    for k in range(len(choices[0])):
        limit = jnp.full((1, LANES), -1.0, jnp.float32)
        for i, choice in enumerate(choices):
            limit = jnp.where(lane[:1] == i, float(choice[k]), limit)
        hits = jnp.sum((source == k + 1).astype(jnp.float32), axis=1, keepdims=True)
        fit = jnp.max(hits, axis=0, keepdims=True) <= limit
        fits = fit if fits is None else fits & fit
    pick = jnp.min(jnp.where(fits, lane[:1].astype(jnp.float32), LANES - 1.0), axis=1, keepdims=True).astype(jnp.int32)
    pick_ref[...] = jnp.broadcast_to(pick, pick_ref.shape)
    lower = (wide(rows[:, steps + 1 : steps + 2]) < wide(mine)) & (row < devices)
    offset = jnp.sum(jnp.where(lower, live, 0).astype(jnp.float32), axis=0, keepdims=True).astype(jnp.int32)
    kind = jnp.maximum(source, 0)
    index = jnp.where(kind > 0, rank, jnp.where(filled, place, 0))
    values = [wide(live[:1]), wide(offset), wide(top_from[:1]), wide(top_place[:1]), start_flag]
    sizes = values[0]
    for i, value in enumerate(values[1:], 1):
        sizes = jnp.where(lane == i, value, sizes)
    sent = jnp.where(lane == capacity, top_place, sent)
    table = jnp.where(row == 0, wide(kind[:1]), jnp.where(row == 1, wide(index[:1]), sizes))
    plan_ref[...] = jnp.where(row > 2, behind(sent, 2), table)


def make_plan(given, choices, capacity, steps):
    devices = given.shape[0]
    count = devices * max(1, SUBLANES // devices)
    return pl.pallas_call(
        functools.partial(plan_kernel, choices=choices, capacity=capacity, steps=steps),
        out_shape=[jax.ShapeDtypeStruct((rows, LANES), jnp.int32) for rows in (count, 1)],
        in_specs=[pl.BlockSpec(memory_space=pltpu.VMEM)],
        out_specs=[pl.BlockSpec(memory_space=pltpu.VMEM)] * 2,
        compiler_params=pltpu.CompilerParams(vmem_limit_bytes=1 << 20),
        name="plan",
    )(given)


def pack_kernel(sizes, last, plan_ref, patches_ref, after_ref, *refs):
    parcels, sems = refs[:-1], refs[-1]
    capacity, parts = patches_ref.shape[:2]

    def each(act):
        used = 0
        for k, (size, parcel) in enumerate(zip(sizes, parcels)):

            @pl.loop(0, size)
            def _(r, k=k, parcel=parcel, used=used):
                act(pltpu.make_async_copy(patches_ref.at[plan_ref[3 + k, r]], parcel.at[pl.ds(r * parts, parts)], sems.at[used + r]))

            used += size
            act(pltpu.make_async_copy(last_plane(patches_ref, plan_ref[3 + k, capacity]), parcel.at[size * parts], sems.at[used]))
            used += 1
            if k == last:
                upper = parcel.at[size * parts + 1]

                @pl.when(plan_ref[2, 4] == 0)
                def _():
                    act(pltpu.make_async_copy(first_plane(patches_ref, 0), upper, sems.at[used]))

                @pl.when(plan_ref[2, 4] != 0)
                def _():
                    act(pltpu.make_async_copy(after_ref, upper, sems.at[used]))

                used += 1

    each(lambda copy: copy.start())
    each(lambda copy: copy.wait())


def pack(plan, patches, after, sizes, last):
    parts = patches.shape[1]
    return pl.pallas_call(
        functools.partial(pack_kernel, sizes, last),
        out_shape=[
            jax.ShapeDtypeStruct((size * parts + 1 + (k == last),) + patches.shape[2:], patches.dtype)
            for k, size in enumerate(sizes)
        ],
        grid_spec=pltpu.PrefetchScalarGridSpec(
            num_scalar_prefetch=1,
            grid=(),
            in_specs=[pl.BlockSpec(memory_space=pl.ANY)] * 2,
            out_specs=[pl.BlockSpec(memory_space=pl.ANY) for _ in sizes],
            scratch_shapes=[pltpu.SemaphoreType.DMA((sum(sizes) + len(sizes) + 1,))],
        ),
        compiler_params=pltpu.CompilerParams(vmem_limit_bytes=1 << 20),
        name="pack",
    )(plan, patches, after)


def settle_kernel(plan_ref, patches_ref, held_ref, sems):
    def each(act):
        @pl.loop(0, held_ref.shape[0])
        def _(j):
            act(pltpu.make_async_copy(patches_ref.at[plan_ref[1, j]], held_ref.at[j], sems.at[j]))

    each(lambda copy: copy.start())
    each(lambda copy: copy.wait())


def settle(plan, patches):
    return pl.pallas_call(
        settle_kernel,
        out_shape=jax.ShapeDtypeStruct(patches.shape, patches.dtype),
        grid_spec=pltpu.PrefetchScalarGridSpec(
            num_scalar_prefetch=1,
            grid=(),
            in_specs=[pl.BlockSpec(memory_space=pl.ANY)],
            out_specs=pl.BlockSpec(memory_space=pl.ANY),
            scratch_shapes=[pltpu.SemaphoreType.DMA((patches.shape[0],))],
        ),
        compiler_params=pltpu.CompilerParams(vmem_limit_bytes=1 << 20),
        cost_estimate=pl.CostEstimate(flops=1 << 24, bytes_accessed=1 << 21, transcendentals=0),
        name="settle",
    )(plan, patches)


def assemble_kernel(sizes, last, plan_ref, patches_ref, after_ref, *refs):
    parcels, work_ref, ends_ref, sems = refs[:-3], refs[-3], refs[-2], refs[-1]
    capacity, parts = work_ref.shape[:2]

    def put(source, side):
        pltpu.make_async_copy(source, ends_ref.at[side], sems.at[capacity + side]).start()

    origin, slot = plan_ref[2, 2], plan_ref[2, 3]
    for k, (size, parcel) in enumerate(zip(sizes, parcels)):

        @pl.when(origin == k + 1)
        def _(parcel=parcel, size=size):
            put(parcel.at[size * parts], 0)

    @pl.when(origin == 0)
    def _():
        put(last_plane(patches_ref, slot), 0)

    put(after_ref if last is None else parcels[last].at[sizes[last] * parts + 1], 1)

    @pl.loop(0, capacity)
    def _(j):
        for k, parcel in enumerate(parcels):

            @pl.when(plan_ref[0, j] == k + 1)
            def _(parcel=parcel):
                pltpu.make_async_copy(parcel.at[pl.ds(plan_ref[1, j] * parts, parts)], work_ref.at[j], sems.at[j]).start()

    for side in (0, 1):
        pltpu.make_async_copy(patches_ref.at[0, 0], ends_ref.at[side], sems.at[capacity + side]).wait()

    @pl.loop(0, capacity)
    def _(j):
        @pl.when(plan_ref[0, j] > 0)
        def _():
            pltpu.make_async_copy(patches_ref.at[0], work_ref.at[j], sems.at[j]).wait()


def assemble(plan, patches, after, arrived, sizes, last):
    return pl.pallas_call(
        functools.partial(assemble_kernel, sizes, last),
        out_shape=[
            jax.ShapeDtypeStruct(patches.shape, patches.dtype),
            jax.ShapeDtypeStruct((2,) + patches.shape[2:], patches.dtype),
        ],
        grid_spec=pltpu.PrefetchScalarGridSpec(
            num_scalar_prefetch=1,
            grid=(),
            in_specs=[pl.BlockSpec(memory_space=pl.ANY) for _ in range(2 + len(arrived))],
            out_specs=[pl.BlockSpec(memory_space=pl.ANY)] * 2,
            scratch_shapes=[pltpu.SemaphoreType.DMA((patches.shape[0] + 2,))],
        ),
        compiler_params=pltpu.CompilerParams(vmem_limit_bytes=1 << 20),
        name="assemble",
    )(plan, patches, after, *arrived)


def exchange(sizes, last, plan, patches, after):
    parcels = pack(plan, patches, after, sizes, last)
    arrived = [forward(parcel, "blk", 1 + k) for k, parcel in enumerate(parcels)]
    return settle(plan, patches), *assemble(plan, patches, after, arrived, sizes, last)


def body(patches, counts, moves, tags):
    capacity, edge, _ = patches.shape
    steps, devices, groups = (moves.shape[1], lax.axis_size("blk"), lax.axis_size("grp"))
    parcels = min(steps + 1, devices - 1)
    choices = capacity_choices(min(steps, devices - 1), capacity)
    parts = tiled(patches)
    mine = lax.axis_index("blk").astype(jnp.int32).reshape(1, 1)
    row = jnp.pad(jnp.concatenate([counts[:, None], moves, mine], 1), ((0, 0), (0, LANES - steps - 2)))
    given = all_of(lax.optimization_barrier(row), "blk")
    first = parts[0, :SUBLANES, 0]
    line = ("grp", "blk")
    if parcels == devices - 1:
        last = parcels - 1
        after = lax.ppermute(first, line, [((g + 1) * devices, g * devices) for g in range(groups - 1)])
    else:
        last = None
        after = lax.ppermute(first, line, [(i + 1, i) for i in range(groups * devices - 1)])
    plan, picks = make_plan(given, choices, capacity, steps)
    pick = jnp.minimum(picks[0, 0], lax.axis_index("grp") + len(choices))
    branches = [functools.partial(exchange, choice + (0,) * (parcels - len(choice)), last) for choice in choices]
    held, work, ends = lax.switch(pick, branches, plan, parts, after)
    before = lax.ppermute(ends[0], line, [(g * devices, (g + 1) * devices) for g in range(groups - 1)])
    return refine(held, work, plan, tags, ends, before, edge)


def solution(mesh):
    in_specs = (
        P(("grp", "blk"), None, None),
        P(("grp", "blk")),
        P(("grp", "blk"), None),
        P("grp", None),
    )
    out_specs = P(("grp", "blk"), None, None)
    return jax.shard_map(body, mesh=mesh, in_specs=in_specs, out_specs=out_specs, check_vma=False)
```

profile of v0, /device:TPU:16, one launch (start us, length us, event | category | flops | bytes accessed | tf_op | source)
XLA Modules:
  0.0 42.6 jit_solution(6875845289751562507)
XLA Ops:
  0.7 0.7 %pad_add_fusion.2 = s32[1,6]{1,0:T(1,128)S(1)} fusion(s32[1,1]{1,0:T(1,128)} %bitcast.1, s32[1,4]{1,0:T(1,128)} %param.44, s32[1,1]{1,0:T(1,128)} %bitcast.14), kind=kLoop, calls=%fused_computation.3 | loop fusion | flops 12 | bytes 48 | tf_op jit(solution)/shard_map/concatenate | solution.py:409
  1.4 1.5 %collective-permute-start.111 = (s32[1,128]{1,0:T(1,128)S(1)}, s32[1,128]{1,0:T(1,128)S(1)}, u32[]{:S(2)}, u32[]{:S(2)}) collective-permute-start(s32[1,128]{1,0:T(1,128)S(1)} %pad.4), channel_id=1, source_target_pairs={{0,1},{1,0},{2,3},{3,2},{4,5},{5,4},{6,7},{7,6},{8,9},{9,8},{10,11... | collective-permute-start | bytes 1544 | tf_op jit(solution)/shard_map/ppermute | solution.py:128
  2.9 2.1 %collective-permute-done.111 = s32[1,128]{1,0:T(1,128)S(1)} collective-permute-done((s32[1,128]{1,0:T(1,128)S(1)}, s32[1,128]{1,0:T(1,128)S(1)}, u32[]{:S(2)}, u32[]{:S(2)}) %collective-permute-start.111) | collective-permute-done | bytes 544 | tf_op jit(solution)/shard_map/ppermute | solution.py:128
  5.0 1.5 %collective-permute-start.112 = (s32[2,128]{1,0:T(2,128)S(1)}, s32[2,128]{1,0:T(2,128)S(1)}, u32[]{:S(2)}, u32[]{:S(2)}) collective-permute-start(s32[2,128]{1,0:T(2,128)S(1)} %pad_add_fusion.1), channel_id=1, source_target_pairs={{0,2},{1,3},{2,0},{3,1},{4,6},{5,7},{6,4},{7,5},{8,10},{9,11},{10,... | collective-permute-start | bytes 3080 | tf_op jit(solution)/shard_map/ppermute | solution.py:128
  6.5 0.8 %slice.12 = f32[1,8,1,128]{3,2,1,0:T(1,128)S(1)} slice(f32[8,32,8,128]{3,2,1,0:T(8,128)} %bitcast.16), slice={[0:1], [0:8], [0:1], [0:128]} | slice | bytes 8192 | tf_op jit(solution)/shard_map/slice | solution.py:411
  7.3 1.9 %collective-permute-start.113 = (f32[8,128]{1,0:T(8,128)S(1)}, f32[8,128]{1,0:T(8,128)S(1)}, u32[]{:S(2)}, u32[]{:S(2)}) collective-permute-start(f32[8,128]{1,0:T(8,128)S(1)} %bitcast.54), channel_id=1, source_target_pairs={{4,0},{8,4},{12,8},{16,12},{20,16},{24,20},{28,24}} | collective-permute-start | bytes 12296 | tf_op jit(solution)/shard_map/ppermute | solution.py:415
  9.2 0.0 collective-permute-done.112
  9.2 0.4 plan.1
  9.7 0.8 %collective-permute-done.113 = f32[8,128]{1,0:T(8,128)S(1)} collective-permute-done((f32[8,128]{1,0:T(8,128)S(1)}, f32[8,128]{1,0:T(8,128)S(1)}, u32[]{:S(2)}, u32[]{:S(2)}) %collective-permute-start.113) | collective-permute-done | bytes 4128 | tf_op jit(solution)/shard_map/ppermute | solution.py:415
  10.5 0.0 copy-start
  10.5 0.0 copy-start.1
  10.5 21.8 %conditional.1 = (f32[8,32,8,128]{3,2,1,0:T(8,128)S(1)}, f32[8,32,8,128]{3,2,1,0:T(8,128)S(1)}, f32[2,8,128]{2,1,0:T(8,128)S(1)}) conditional(s32[]{:T(128)} %clamp.3, (s32[8,128]{1,0:T(8,128)S(1)}, f32[8,32,8,128]{3,2,1,0:T(8,128)}, f32[8,128]{1,0:T(8,128)S(1)}) %tuple.208, (s32[8,128]{1,0:T(8,128)S(1)}, ...), branch_computations={%region_0.1_spmd, %region_1.2_spmd, %region_2.3_spmd, %region_3.4_... | conditional | flops 16777216 | bytes 13172880 | solution.py:422
  10.5 2.0 %pack.56 = (f32[33,8,128]{2,1,0:T(8,128)S(1)}, f32[161,8,128]{2,1,0:T(8,128)S(1)}, f32[34,8,128]{2,1,0:T(8,128)S(1)}) custom-call(s32[8,128]{1,0:T(8,128)S(1)} %get-tuple-element.379.plan_ref, f32[8,32,8,128]{3,2,1,0:T(8,128)} %get-tuple-element.380.patches_ref, f32[8,128]{1,0:T(8,128)S(1)} %get-tuple-element.381.after_ref), custom_call_target="tpu_custom_call" | custom-call | tf_op jit(solution)/shard_map/cond/branch_19_fun/pack/pallas_call | solution.py:294
  12.5 0.2 collective-permute-start.58
  12.7 1.5 %collective-permute-start.59 = (f32[34,8,128]{2,1,0:T(8,128)S(1)}, f32[34,8,128]{2,1,0:T(8,128)S(1)}, u32[]{:S(2)}, u32[]{:S(2)}) collective-permute-start(f32[34,8,128]{2,1,0:T(8,128)S(1)} %get-tuple-element.384), channel_id=1, source_target_pairs={{0,3},{1,0},{2,1},{3,2},{4,7},{5,4},{6,5},{7,6},{8,11},{9,8},{10,9... | collective-permute-start | bytes 417800 | tf_op jit(solution)/shard_map/cond/branch_19_fun/ppermute | solution.py:142
  14.2 0.5 %collective-permute-start.57 = (f32[33,8,128]{2,1,0:T(8,128)S(1)}, f32[33,8,128]{2,1,0:T(8,128)S(1)}, u32[]{:S(2)}, u32[]{:S(2)}) collective-permute-start(f32[33,8,128]{2,1,0:T(8,128)S(1)} %get-tuple-element.382), channel_id=1, source_target_pairs={{0,1},{1,2},{2,3},{3,0},{4,5},{5,6},{6,7},{7,4},{8,9},{9,10},{10,1... | collective-permute-start | bytes 405512 | tf_op jit(solution)/shard_map/cond/branch_19_fun/ppermute | solution.py:142
  14.7 2.0 %settle.56 = f32[8,32,8,128]{3,2,1,0:T(8,128)S(1)} custom-call(s32[8,128]{1,0:T(8,128)S(1)} %get-tuple-element.379.plan_ref, f32[8,32,8,128]{3,2,1,0:T(8,128)} %get-tuple-element.380.patches_ref), custom_call_target="tpu_custom_call" | custom-call | flops 16777216 | bytes 2097152 | tf_op jit(solution)/shard_map/cond/branch_19_fun/settle/pallas_call | solution.py:323
  16.8 6.5 %collective-permute-done.57.refs_0_ = f32[33,8,128]{2,1,0:T(8,128)S(1)} collective-permute-done((f32[33,8,128]{2,1,0:T(8,128)S(1)}, f32[33,8,128]{2,1,0:T(8,128)S(1)}, u32[]{:S(2)}, u32[]{:S(2)}) %collective-permute-start.57) | collective-permute-done | bytes 135200 | tf_op jit(solution)/shard_map/cond/branch_19_fun/ppermute | solution.py:142
  23.3 0.0 collective-permute-done.59.refs_2_
  23.3 7.1 %collective-permute-done.58.refs_1_ = f32[161,8,128]{2,1,0:T(8,128)S(1)} collective-permute-done((f32[161,8,128]{2,1,0:T(8,128)S(1)}, f32[161,8,128]{2,1,0:T(8,128)S(1)}, u32[]{:S(2)}, u32[]{:S(2)}) %collective-permute-start.58) | collective-permute-done | bytes 659488 | tf_op jit(solution)/shard_map/cond/branch_19_fun/ppermute | solution.py:142
  30.3 1.5 %assemble.56 = (f32[8,32,8,128]{3,2,1,0:T(8,128)S(1)}, f32[2,8,128]{2,1,0:T(8,128)S(1)}) custom-call(s32[8,128]{1,0:T(8,128)S(1)} %get-tuple-element.379.plan_ref, f32[8,32,8,128]{3,2,1,0:T(8,128)} %get-tuple-element.380.patches_ref, f32[8,128]{1,0:T(8,128)S(1)} %get-tuple-element.381.after_ref, f32[33,8,128]{2,1,0:T(8,128)S(1)} %collective-permute-done.57.refs_0_, ...), custom_call_target="tpu_custom_call" | custom-call | tf_op jit(solution)/shard_map/cond/branch_19_fun/assemble/pallas_call | solution.py:378
  32.3 1.9 %collective-permute-start.114 = (f32[8,128]{1,0:T(8,128)S(1)}, f32[8,128]{1,0:T(8,128)S(1)}, u32[]{:S(2)}, u32[]{:S(2)}) collective-permute-start(f32[8,128]{1,0:T(8,128)S(1)} %slice_bitcast_fusion), channel_id=1, source_target_pairs={{0,4},{4,8},{8,12},{12,16},{16,20},{20,24},{24,28}} | collective-permute-start | bytes 12296 | tf_op jit(solution)/shard_map/ppermute | solution.py:423
  34.2 3.0 %collective-permute-done.114.before_ref = f32[8,128]{1,0:T(8,128)S(1)} collective-permute-done((f32[8,128]{1,0:T(8,128)S(1)}, f32[8,128]{1,0:T(8,128)S(1)}, u32[]{:S(2)}, u32[]{:S(2)}) %collective-permute-start.114) | collective-permute-done | bytes 4128 | tf_op jit(solution)/shard_map/ppermute | solution.py:423
  37.2 0.0 copy-done
  37.2 0.0 copy-done.1
  37.2 5.4 %refine.1 = bf16[8,64,4096]{2,1,0:T(8,128)(2,1)} custom-call(s32[8,128]{1,0:T(8,128)S(1)} %get-tuple-element.528.plan_ref, s32[1,32]{1,0:T(1,128)S(1)} %copy-done.1, f32[8,32,8,128]{3,2,1,0:T(8,128)S(1)} %get-tuple-element.530.held_ref, f32[8,32,8,128]{3,2,1,0:T(8,128)S(1)} %get-tuple-element.531.work_ref, f32[2,8,128]{2,1,0:T(8,128)S(1)} %get-tuple-element.532.ends_ref, ...), custom_call_target="tpu_custom_call" | custom-call | tf_op jit(solution)/shard_map/refine/pallas_call | solution.py:109
  (4 shorter events, 0.0 us)
Async XLA Ops:
  1.4 3.6 %collective-permute-start.111 = (s32[1,128]{1,0:T(1,128)S(1)}, s32[1,128]{1,0:T(1,128)S(1)}, u32[]{:S(2)}, u32[]{:S(2)}) collective-permute-start(s32[1,128]{1,0:T(1,128)S(1)} %pad.4), channel_id=1, source_target_pairs={{0,1},{1,0},{2,3},{3,2},{4,5},{5,4},{6,7},{7,6},{8,9},{9,8},{10,11... | collective-permute-start | bytes 1544 | tf_op jit(solution)/shard_map/ppermute | solution.py:128
  5.0 4.2 %collective-permute-start.112 = (s32[2,128]{1,0:T(2,128)S(1)}, s32[2,128]{1,0:T(2,128)S(1)}, u32[]{:S(2)}, u32[]{:S(2)}) collective-permute-start(s32[2,128]{1,0:T(2,128)S(1)} %pad_add_fusion.1), channel_id=1, source_target_pairs={{0,2},{1,3},{2,0},{3,1},{4,6},{5,7},{6,4},{7,5},{8,10},{9,11},{10,... | collective-permute-start | bytes 3080 | tf_op jit(solution)/shard_map/ppermute | solution.py:128
  7.3 3.2 %collective-permute-start.113 = (f32[8,128]{1,0:T(8,128)S(1)}, f32[8,128]{1,0:T(8,128)S(1)}, u32[]{:S(2)}, u32[]{:S(2)}) collective-permute-start(f32[8,128]{1,0:T(8,128)S(1)} %bitcast.54), channel_id=1, source_target_pairs={{4,0},{8,4},{12,8},{16,12},{20,16},{24,20},{28,24}} | collective-permute-start | bytes 12296 | tf_op jit(solution)/shard_map/ppermute | solution.py:415
  10.5 26.8 %copy-start = (bf16[256,256]{1,0:T(8,128)(2,1)S(1)}, bf16[256,256]{1,0:T(8,128)(2,1)}, u32[]{:S(2)}) copy-start(bf16[256,256]{1,0:T(8,128)(2,1)} %constant.17.clone.table_ref) | copy-start | bytes 393220
  10.5 26.8 %copy-start.1 = (s32[1,32]{1,0:T(1,128)S(1)}, s32[1,32]{1,0:T(1,128)}, u32[]{:S(2)}) copy-start(s32[1,32]{1,0:T(1,128)} %tag_ref.1) | copy-start | bytes 388
  12.5 17.8 %collective-permute-start.58 = (f32[161,8,128]{2,1,0:T(8,128)S(1)}, f32[161,8,128]{2,1,0:T(8,128)S(1)}, u32[]{:S(2)}, u32[]{:S(2)}) collective-permute-start(f32[161,8,128]{2,1,0:T(8,128)S(1)} %get-tuple-element.383), channel_id=1, source_target_pairs={{0,2},{1,3},{2,0},{3,1},{4,6},{5,7},{6,4},{7,5},{8,10},{9,11},{10,... | collective-permute-start | bytes 1978376 | tf_op jit(solution)/shard_map/cond/branch_19_fun/ppermute | solution.py:142
  12.7 10.6 %collective-permute-start.59 = (f32[34,8,128]{2,1,0:T(8,128)S(1)}, f32[34,8,128]{2,1,0:T(8,128)S(1)}, u32[]{:S(2)}, u32[]{:S(2)}) collective-permute-start(f32[34,8,128]{2,1,0:T(8,128)S(1)} %get-tuple-element.384), channel_id=1, source_target_pairs={{0,3},{1,0},{2,1},{3,2},{4,7},{5,4},{6,5},{7,6},{8,11},{9,8},{10,9... | collective-permute-start | bytes 417800 | tf_op jit(solution)/shard_map/cond/branch_19_fun/ppermute | solution.py:142
  14.2 9.0 %collective-permute-start.57 = (f32[33,8,128]{2,1,0:T(8,128)S(1)}, f32[33,8,128]{2,1,0:T(8,128)S(1)}, u32[]{:S(2)}, u32[]{:S(2)}) collective-permute-start(f32[33,8,128]{2,1,0:T(8,128)S(1)} %get-tuple-element.382), channel_id=1, source_target_pairs={{0,1},{1,2},{2,3},{3,0},{4,5},{5,6},{6,7},{7,4},{8,9},{9,10},{10,1... | collective-permute-start | bytes 405512 | tf_op jit(solution)/shard_map/cond/branch_19_fun/ppermute | solution.py:142
  32.3 4.9 %collective-permute-start.114 = (f32[8,128]{1,0:T(8,128)S(1)}, f32[8,128]{1,0:T(8,128)S(1)}, u32[]{:S(2)}, u32[]{:S(2)}) collective-permute-start(f32[8,128]{1,0:T(8,128)S(1)} %slice_bitcast_fusion), channel_id=1, source_target_pairs={{0,4},{4,8},{8,12},{12,16},{16,20},{20,24},{24,28}} | collective-permute-start | bytes 12296 | tf_op jit(solution)/shard_map/ppermute | solution.py:423
where the time goes:
time: 42.9 us; the launch traced here: 42.6 us
  waiting for transfers between devices  19.4 us (45%)
  Pallas kernels  11.3 us (26%)
  starting transfers between devices  9.1 us (21%)
  local copies, waits for them, and re-layouts  0.78 us (2%)
  between operations  0.77 us (2%)
  other arithmetic  0.75 us (2%)
  loops' own time  0.45 us (1%)
    ppermute x3, waiting for transfers between devices, forward(): lax.ppermute(block, axis, [(i, (i + distance) % count) for i in range(cou...  13.6 us
    pallas_call x1, Pallas kernels, refine(): pl.pallas_call(refine_kernel, out_shape=jax.ShapeDtypeStruct((capacity, 2...  5.36 us
    ppermute x2, starting transfers between devices, swap(): lax.ppermute(block, axis, [(i, i ^ bit) for i in range(lax.axis_size(axis...  3.02 us
    ppermute x1, waiting for transfers between devices, body(): lax.ppermute(ends[0], line, [(g * devices, (g + 1) * devices) for g in ra...  3 us
    ppermute x3, starting transfers between devices, forward(): lax.ppermute(block, axis, [(i, (i + distance) % count) for i in range(cou...  2.24 us
    ppermute x2, waiting for transfers between devices, swap(): lax.ppermute(block, axis, [(i, i ^ bit) for i in range(lax.axis_size(axis...  2.08 us
    pallas_call x1, Pallas kernels, settle(): pl.pallas_call(settle_kernel, out_shape=jax.ShapeDtypeStruct(patches.shap...  2.03 us
    pallas_call x1, Pallas kernels, pack(): pl.pallas_call(functools.partial(pack_kernel, sizes, last), out_shape=[ja...  1.98 us
  transfers between devices with their start and end apart: 7, of which 5 were waited for; matrix products, arithmetic and copies ran while one was open for 2% of the time, Pallas kernels for 6%

commit v1 on v0

--- a/solution.py
+++ b/solution.py
@@ -12,6 +12,7 @@
 
 LANES = 128
 SUBLANES = 8
+TOGETHER = 2
 CHOICES = (
     (4, 3, 3), (5, 4, 4), (3, 2, 2), (2, 4, 2), (2, 2, 2), (3, 5, 3), (3, 3, 3), (5, 2, 2), (4, 2, 2),
     (2, 3, 2), (2, 2, 3), (4, 1, 1), (1, 3, 1), (1, 1, 2), (3, 1, 1), (5, 1, 1), (1, 2, 1), (2, 2, 4),
@@ -36,74 +37,85 @@
     return jnp.asarray(np.concatenate([table, table], 0), jnp.bfloat16)
 
 
-def refine_kernel(plan_ref, tag_ref, held_ref, work_ref, ends_ref, before_ref, table_ref, out_ref, rows_ref, split_ref):
-    capacity = work_ref.shape[0]
-    fine = out_ref.shape[1]
-    edge, plane = (fine // 2, out_ref.shape[2] // 4)
+def flat(tiles, across):
+    tiles = tiles.reshape(-1, across, tiles.shape[-2], LANES)
+    return jnp.concatenate([tiles[:, u].reshape(-1, LANES) for u in range(across)], axis=1)
+
+
+def refined(middle, before, after, factor, edge, table, rows_ref, put):
+    coarse, plane = middle.shape
     across = plane // LANES
-    slot = pl.program_id(0)
+    place = lax.broadcasted_iota(jnp.int32, middle.shape, 0)
+    below = jnp.where(place == 0, before, pltpu.roll(middle, 1, 0))
+    above = jnp.where(place == coarse - 1, after, pltpu.roll(middle, coarse - 1, 0))
+    home = middle * (0.75 * factor)
+    even = home + below * (0.25 * factor)
+    odd = home + above * (0.25 * factor)
+    for u in range(across):
+        cut = slice(u * LANES, (u + 1) * LANES)
+        rows_ref[u, pl.ds(0, coarse, 2), :] = even[:, cut]
+        rows_ref[u, pl.ds(1, coarse, 2), :] = odd[:, cut]
+    rows = jnp.concatenate([rows_ref[u, : 2 * coarse] for u in range(across)], axis=1)
+    lane = lax.broadcasted_iota(jnp.int32, rows.shape, 1)
+    later = jnp.where(lane < edge, 0.0, pltpu.roll(rows, edge, 1))
+    sooner = jnp.where(lane >= plane - edge, 0.0, pltpu.roll(rows, plane - edge, 1))
+    width = table.shape[1]
+    pairs = []
+    for moved in (later, sooner):
+        high = moved.astype(jnp.bfloat16)
+        pairs.append((high, (moved - high.astype(jnp.float32)).astype(jnp.bfloat16)))
+    for window in range(2 * across):
+        cut = slice(window // 2 * LANES, (window // 2 + 1) * LANES)
+        left = jnp.concatenate([half[:, cut] for half in pairs[window % 2]], axis=1)
+        product = jnp.dot(left, table, preferred_element_type=jnp.float32)
+        put(slice(window * width, (window + 1) * width), product.astype(jnp.bfloat16))
+
+
+def tag_factor(plan_ref, tag_ref, slot):
+    return 1.0 + 0.5 * tag_ref[0, plan_ref[2, 1] + slot].astype(jnp.float32)
+
+
+def refine_kernel(plan_ref, tag_ref, held_ref, work_ref, ends_ref, before_ref, table_ref, out_ref, rows_ref):
+    capacity, parts = held_ref.shape[:2]
+    together, fine, wide = out_ref.shape
+    edge, across = (fine // 2, wide // 4 // LANES)
+    base = pl.program_id(0) * together
     live = plan_ref[2, 0]
 
-    @pl.when(slot >= live)
+    @pl.when(base >= live)
     def _():
         out_ref[...] = jnp.zeros_like(out_ref)
 
-    @pl.when(slot < live)
+    @pl.when(base < live)
     def _():
-        factor = 1.0 + 0.5 * tag_ref[0, plan_ref[2, 1] + slot].astype(jnp.float32)
-
         def part(j, tiles, rows):
             j = jnp.clip(j, 0, capacity - 1)
             return jnp.where(plan_ref[0, j] == 0, held_ref[j, tiles, rows], work_ref[j, tiles, rows])
 
-        def flat(tiles):
-            tiles = tiles.reshape(-1, across, tiles.shape[-2], LANES)
-            return jnp.concatenate([tiles[:, u].reshape(-1, LANES) for u in range(across)], axis=1)
-
-        middle = flat(part(slot, slice(None), slice(None)))
-        before = part(slot - 1, slice(edge // SUBLANES * across - across, None), slice(SUBLANES - 1, None))
-        after = part(slot + 1, slice(0, across), slice(0, 1))
-        lower = jnp.where(plan_ref[2, 4] == 0, ends_ref[0], before_ref[...])
-        before = jnp.where(slot == 0, lower[:, None, :], before)
-        after = jnp.where(slot == live - 1, ends_ref[1][:, None, :], after)
-        before, after = flat(before), flat(after)
-        place = lax.broadcasted_iota(jnp.int32, middle.shape, 0)
-        below = jnp.where(place == 0, before, pltpu.roll(middle, 1, 0))
-        above = jnp.where(place == edge - 1, after, pltpu.roll(middle, edge - 1, 0))
-        home = middle * (0.75 * factor)
-        even = home + below * (0.25 * factor)
-        odd = home + above * (0.25 * factor)
-        for u in range(plane // LANES):
-            cut = slice(u * LANES, (u + 1) * LANES)
-            rows_ref[u, pl.ds(0, edge, 2), :] = even[:, cut]
-            rows_ref[u, pl.ds(1, edge, 2), :] = odd[:, cut]
-        rows = jnp.concatenate([rows_ref[u] for u in range(plane // LANES)], axis=1)
-        lane = lax.broadcasted_iota(jnp.int32, rows.shape, 1)
-        later = jnp.where(lane < edge, 0.0, pltpu.roll(rows, edge, 1))
-        sooner = jnp.where(lane >= plane - edge, 0.0, pltpu.roll(rows, plane - edge, 1))
-        for side, moved in enumerate((later, sooner)):
-            high = moved.astype(jnp.bfloat16)
-            low = (moved - high.astype(jnp.float32)).astype(jnp.bfloat16)
-            for u in range(plane // LANES):
-                cut = slice(u * LANES, (u + 1) * LANES)
-                split_ref[2 * u + side, :, :LANES] = high[:, cut]
-                split_ref[2 * u + side, :, LANES:] = low[:, cut]
-        windows, fine, depth = split_ref.shape
-        width = table_ref.shape[1]
         table = table_ref[...]
-        group = 4
-        for g in range(0, windows, group):
-            left = split_ref[g : g + group].reshape(group * fine, depth)
-            product = jnp.dot(left, table, preferred_element_type=jnp.float32)
-            for i in range(group):
-                out_ref[0, :, (g + i) * width : (g + i + 1) * width] = product[i * fine : (i + 1) * fine].astype(jnp.bfloat16)
+        lower = jnp.where(plan_ref[2, 4] == 0, ends_ref[0], before_ref[...])[:, None, :]
+        for t in range(together):
+            slot = base + t
+            middle = part(slot, slice(None), slice(None))
+            before = part(slot - 1, slice(parts - across, None), slice(SUBLANES - 1, None))
+            after = part(slot + 1, slice(0, across), slice(0, 1))
+            before = jnp.where(slot == 0, lower, before)
+            after = jnp.where(slot == live - 1, ends_ref[1][:, None, :], after)
+            factor = tag_factor(plan_ref, tag_ref, jnp.minimum(slot, live - 1))
+            if t:
+                middle, before, after = (jnp.where(slot < live, x, 0.0) for x in (middle, before, after))
+
+            def put(lanes, values, t=t):
+                out_ref[t, :, lanes] = values
+
+            refined(flat(middle, across), flat(before, across), flat(after, across), factor, edge, table, rows_ref.at[t], put)
 
 
 def refine(held, work, plan, tags, ends, before, edge):
     capacity, parts = work.shape[:2]
     plane = parts * SUBLANES * LANES // edge
     table = window_table(edge)
-    windows = 2 * plane // LANES
+    together = TOGETHER if capacity % TOGETHER == 0 else 1
     whole = lambda x: pl.BlockSpec(x.shape, lambda i, *_: (0,) * x.ndim)
     operands = (held, work, ends, before, table)
     return pl.pallas_call(
@@ -111,13 +123,10 @@
         out_shape=jax.ShapeDtypeStruct((capacity, 2 * edge, 4 * plane), jnp.bfloat16),
         grid_spec=pltpu.PrefetchScalarGridSpec(
             num_scalar_prefetch=2,
-            grid=(capacity,),
+            grid=(capacity // together,),
             in_specs=[whole(x) for x in operands],
-            out_specs=pl.BlockSpec((1, 2 * edge, 4 * plane), lambda i, *_: (i, 0, 0)),
-            scratch_shapes=[
-                pltpu.VMEM((plane // LANES, 2 * edge, LANES), jnp.float32),
-                pltpu.VMEM((windows, 2 * edge, 2 * LANES), jnp.bfloat16),
-            ],
+            out_specs=pl.BlockSpec((together, 2 * edge, 4 * plane), lambda i, *_: (i, 0, 0)),
+            scratch_shapes=[pltpu.VMEM((together, plane // LANES, 2 * edge, LANES), jnp.float32)],
         ),
         compiler_params=pltpu.CompilerParams(vmem_limit_bytes=16 << 20),
         name="refine",

time: 42.9 us -> 42.3 us (0.986)
  Pallas kernels: 11.3 us -> 10.7 us
    pallas_call x1, Pallas kernels: 5.36 us -> 4.78 us  [refine(): pl.pallas_call(refine_kernel, out_shape=jax.ShapeDtypeStruct((capacity, 2...]
where the time goes in v1:
time: 42.3 us; the launch traced here: 42 us
  waiting for transfers between devices  19.4 us (46%)
  Pallas kernels  10.7 us (25%)
  starting transfers between devices  9.1 us (22%)
  local copies, waits for them, and re-layouts  0.78 us (2%)
  between operations  0.77 us (2%)
  other arithmetic  0.75 us (2%)
  loops' own time  0.45 us (1%)
    ppermute x3, waiting for transfers between devices, forward(): lax.ppermute(block, axis, [(i, (i + distance) % count) for i in range(cou...  13.6 us
    pallas_call x1, Pallas kernels, refine(): pl.pallas_call(refine_kernel, out_shape=jax.ShapeDtypeStruct((capacity, 2...  4.78 us
    ppermute x2, starting transfers between devices, swap(): lax.ppermute(block, axis, [(i, i ^ bit) for i in range(lax.axis_size(axis...  3.02 us
    ppermute x1, waiting for transfers between devices, body(): lax.ppermute(ends[0], line, [(g * devices, (g + 1) * devices) for g in ra...  3 us
    ppermute x3, starting transfers between devices, forward(): lax.ppermute(block, axis, [(i, (i + distance) % count) for i in range(cou...  2.24 us
    ppermute x2, waiting for transfers between devices, swap(): lax.ppermute(block, axis, [(i, i ^ bit) for i in range(lax.axis_size(axis...  2.08 us
    pallas_call x1, Pallas kernels, settle(): pl.pallas_call(settle_kernel, out_shape=jax.ShapeDtypeStruct(patches.shap...  2.03 us
    pallas_call x1, Pallas kernels, pack(): pl.pallas_call(functools.partial(pack_kernel, sizes, last), out_shape=[ja...  1.98 us
  transfers between devices with their start and end apart: 7, of which 5 were waited for; matrix products, arithmetic and copies ran while one was open for 2% of the time, Pallas kernels for 6%

profile of v1, /device:TPU:16, one launch (start us, length us, event | category | flops | bytes accessed | tf_op | source)
XLA Modules:
  0.0 42.0 jit_solution(15662915217727296123)
XLA Ops:
  0.7 0.7 %pad_add_fusion.2 = s32[1,6]{1,0:T(1,128)S(1)} fusion(s32[1,1]{1,0:T(1,128)} %bitcast.1, s32[1,4]{1,0:T(1,128)} %param.44, s32[1,1]{1,0:T(1,128)} %bitcast.14), kind=kLoop, calls=%fused_computation.3 | loop fusion | flops 12 | bytes 48 | tf_op jit(solution)/shard_map/concatenate | solution.py:418
  1.4 1.5 %collective-permute-start.111 = (s32[1,128]{1,0:T(1,128)S(1)}, s32[1,128]{1,0:T(1,128)S(1)}, u32[]{:S(2)}, u32[]{:S(2)}) collective-permute-start(s32[1,128]{1,0:T(1,128)S(1)} %pad.4), channel_id=1, source_target_pairs={{0,1},{1,0},{2,3},{3,2},{4,5},{5,4},{6,7},{7,6},{8,9},{9,8},{10,11... | collective-permute-start | bytes 1544 | tf_op jit(solution)/shard_map/ppermute | solution.py:137
  2.9 2.1 %collective-permute-done.111 = s32[1,128]{1,0:T(1,128)S(1)} collective-permute-done((s32[1,128]{1,0:T(1,128)S(1)}, s32[1,128]{1,0:T(1,128)S(1)}, u32[]{:S(2)}, u32[]{:S(2)}) %collective-permute-start.111) | collective-permute-done | bytes 544 | tf_op jit(solution)/shard_map/ppermute | solution.py:137
  5.0 1.5 %collective-permute-start.112 = (s32[2,128]{1,0:T(2,128)S(1)}, s32[2,128]{1,0:T(2,128)S(1)}, u32[]{:S(2)}, u32[]{:S(2)}) collective-permute-start(s32[2,128]{1,0:T(2,128)S(1)} %pad_add_fusion.1), channel_id=1, source_target_pairs={{0,2},{1,3},{2,0},{3,1},{4,6},{5,7},{6,4},{7,5},{8,10},{9,11},{10,... | collective-permute-start | bytes 3080 | tf_op jit(solution)/shard_map/ppermute | solution.py:137
  6.5 0.8 %slice.12 = f32[1,8,1,128]{3,2,1,0:T(1,128)S(1)} slice(f32[8,32,8,128]{3,2,1,0:T(8,128)} %bitcast.16), slice={[0:1], [0:8], [0:1], [0:128]} | slice | bytes 8192 | tf_op jit(solution)/shard_map/slice | solution.py:420
  7.3 1.9 %collective-permute-start.113 = (f32[8,128]{1,0:T(8,128)S(1)}, f32[8,128]{1,0:T(8,128)S(1)}, u32[]{:S(2)}, u32[]{:S(2)}) collective-permute-start(f32[8,128]{1,0:T(8,128)S(1)} %bitcast.54), channel_id=1, source_target_pairs={{4,0},{8,4},{12,8},{16,12},{20,16},{24,20},{28,24}} | collective-permute-start | bytes 12296 | tf_op jit(solution)/shard_map/ppermute | solution.py:424
  9.2 0.0 collective-permute-done.112
  9.2 0.4 plan.1
  9.7 0.8 %collective-permute-done.113 = f32[8,128]{1,0:T(8,128)S(1)} collective-permute-done((f32[8,128]{1,0:T(8,128)S(1)}, f32[8,128]{1,0:T(8,128)S(1)}, u32[]{:S(2)}, u32[]{:S(2)}) %collective-permute-start.113) | collective-permute-done | bytes 4128 | tf_op jit(solution)/shard_map/ppermute | solution.py:424
  10.5 0.0 copy-start
  10.5 0.0 copy-start.1
  10.5 21.8 %conditional.1 = (f32[8,32,8,128]{3,2,1,0:T(8,128)S(1)}, f32[8,32,8,128]{3,2,1,0:T(8,128)S(1)}, f32[2,8,128]{2,1,0:T(8,128)S(1)}) conditional(s32[]{:T(128)} %clamp.3, (s32[8,128]{1,0:T(8,128)S(1)}, f32[8,32,8,128]{3,2,1,0:T(8,128)}, f32[8,128]{1,0:T(8,128)S(1)}) %tuple.208, (s32[8,128]{1,0:T(8,128)S(1)}, ...), branch_computations={%region_0.1_spmd, %region_1.2_spmd, %region_2.3_spmd, %region_3.4_... | conditional | flops 16777216 | bytes 13172880 | solution.py:431
  10.5 2.0 %pack.56 = (f32[33,8,128]{2,1,0:T(8,128)S(1)}, f32[161,8,128]{2,1,0:T(8,128)S(1)}, f32[34,8,128]{2,1,0:T(8,128)S(1)}) custom-call(s32[8,128]{1,0:T(8,128)S(1)} %get-tuple-element.379.plan_ref, f32[8,32,8,128]{3,2,1,0:T(8,128)} %get-tuple-element.380.patches_ref, f32[8,128]{1,0:T(8,128)S(1)} %get-tuple-element.381.after_ref), custom_call_target="tpu_custom_call" | custom-call | tf_op jit(solution)/shard_map/cond/branch_19_fun/pack/pallas_call | solution.py:303
  12.5 0.2 collective-permute-start.58
  12.7 1.5 %collective-permute-start.59 = (f32[34,8,128]{2,1,0:T(8,128)S(1)}, f32[34,8,128]{2,1,0:T(8,128)S(1)}, u32[]{:S(2)}, u32[]{:S(2)}) collective-permute-start(f32[34,8,128]{2,1,0:T(8,128)S(1)} %get-tuple-element.384), channel_id=1, source_target_pairs={{0,3},{1,0},{2,1},{3,2},{4,7},{5,4},{6,5},{7,6},{8,11},{9,8},{10,9... | collective-permute-start | bytes 417800 | tf_op jit(solution)/shard_map/cond/branch_19_fun/ppermute | solution.py:151
  14.2 0.5 %collective-permute-start.57 = (f32[33,8,128]{2,1,0:T(8,128)S(1)}, f32[33,8,128]{2,1,0:T(8,128)S(1)}, u32[]{:S(2)}, u32[]{:S(2)}) collective-permute-start(f32[33,8,128]{2,1,0:T(8,128)S(1)} %get-tuple-element.382), channel_id=1, source_target_pairs={{0,1},{1,2},{2,3},{3,0},{4,5},{5,6},{6,7},{7,4},{8,9},{9,10},{10,1... | collective-permute-start | bytes 405512 | tf_op jit(solution)/shard_map/cond/branch_19_fun/ppermute | solution.py:151
  14.7 2.0 %settle.56 = f32[8,32,8,128]{3,2,1,0:T(8,128)S(1)} custom-call(s32[8,128]{1,0:T(8,128)S(1)} %get-tuple-element.379.plan_ref, f32[8,32,8,128]{3,2,1,0:T(8,128)} %get-tuple-element.380.patches_ref), custom_call_target="tpu_custom_call" | custom-call | flops 16777216 | bytes 2097152 | tf_op jit(solution)/shard_map/cond/branch_19_fun/settle/pallas_call | solution.py:332
  16.8 6.5 %collective-permute-done.57.refs_0_ = f32[33,8,128]{2,1,0:T(8,128)S(1)} collective-permute-done((f32[33,8,128]{2,1,0:T(8,128)S(1)}, f32[33,8,128]{2,1,0:T(8,128)S(1)}, u32[]{:S(2)}, u32[]{:S(2)}) %collective-permute-start.57) | collective-permute-done | bytes 135200 | tf_op jit(solution)/shard_map/cond/branch_19_fun/ppermute | solution.py:151
  23.3 0.0 collective-permute-done.59.refs_2_
  23.3 7.1 %collective-permute-done.58.refs_1_ = f32[161,8,128]{2,1,0:T(8,128)S(1)} collective-permute-done((f32[161,8,128]{2,1,0:T(8,128)S(1)}, f32[161,8,128]{2,1,0:T(8,128)S(1)}, u32[]{:S(2)}, u32[]{:S(2)}) %collective-permute-start.58) | collective-permute-done | bytes 659488 | tf_op jit(solution)/shard_map/cond/branch_19_fun/ppermute | solution.py:151
  30.3 1.5 %assemble.56 = (f32[8,32,8,128]{3,2,1,0:T(8,128)S(1)}, f32[2,8,128]{2,1,0:T(8,128)S(1)}) custom-call(s32[8,128]{1,0:T(8,128)S(1)} %get-tuple-element.379.plan_ref, f32[8,32,8,128]{3,2,1,0:T(8,128)} %get-tuple-element.380.patches_ref, f32[8,128]{1,0:T(8,128)S(1)} %get-tuple-element.381.after_ref, f32[33,8,128]{2,1,0:T(8,128)S(1)} %collective-permute-done.57.refs_0_, ...), custom_call_target="tpu_custom_call" | custom-call | tf_op jit(solution)/shard_map/cond/branch_19_fun/assemble/pallas_call | solution.py:387
  32.3 1.9 %collective-permute-start.114 = (f32[8,128]{1,0:T(8,128)S(1)}, f32[8,128]{1,0:T(8,128)S(1)}, u32[]{:S(2)}, u32[]{:S(2)}) collective-permute-start(f32[8,128]{1,0:T(8,128)S(1)} %slice_bitcast_fusion), channel_id=1, source_target_pairs={{0,4},{4,8},{8,12},{12,16},{16,20},{20,24},{24,28}} | collective-permute-start | bytes 12296 | tf_op jit(solution)/shard_map/ppermute | solution.py:432
  34.2 3.0 %collective-permute-done.114.before_ref = f32[8,128]{1,0:T(8,128)S(1)} collective-permute-done((f32[8,128]{1,0:T(8,128)S(1)}, f32[8,128]{1,0:T(8,128)S(1)}, u32[]{:S(2)}, u32[]{:S(2)}) %collective-permute-start.114) | collective-permute-done | bytes 4128 | tf_op jit(solution)/shard_map/ppermute | solution.py:432
  37.2 0.0 copy-done
  37.2 0.0 copy-done.1
  37.2 4.8 %refine.1 = bf16[8,64,4096]{2,1,0:T(8,128)(2,1)} custom-call(s32[8,128]{1,0:T(8,128)S(1)} %get-tuple-element.528.plan_ref, s32[1,32]{1,0:T(1,128)S(1)} %copy-done.1, f32[8,32,8,128]{3,2,1,0:T(8,128)S(1)} %get-tuple-element.530.held_ref, f32[8,32,8,128]{3,2,1,0:T(8,128)S(1)} %get-tuple-element.531.work_ref, f32[2,8,128]{2,1,0:T(8,128)S(1)} %get-tuple-element.532.ends_ref, ...), custom_call_target="tpu_custom_call" | custom-call | tf_op jit(solution)/shard_map/refine/pallas_call | solution.py:121
  (4 shorter events, 0.0 us)
Async XLA Ops:
  1.4 3.6 %collective-permute-start.111 = (s32[1,128]{1,0:T(1,128)S(1)}, s32[1,128]{1,0:T(1,128)S(1)}, u32[]{:S(2)}, u32[]{:S(2)}) collective-permute-start(s32[1,128]{1,0:T(1,128)S(1)} %pad.4), channel_id=1, source_target_pairs={{0,1},{1,0},{2,3},{3,2},{4,5},{5,4},{6,7},{7,6},{8,9},{9,8},{10,11... | collective-permute-start | bytes 1544 | tf_op jit(solution)/shard_map/ppermute | solution.py:137
  5.0 4.2 %collective-permute-start.112 = (s32[2,128]{1,0:T(2,128)S(1)}, s32[2,128]{1,0:T(2,128)S(1)}, u32[]{:S(2)}, u32[]{:S(2)}) collective-permute-start(s32[2,128]{1,0:T(2,128)S(1)} %pad_add_fusion.1), channel_id=1, source_target_pairs={{0,2},{1,3},{2,0},{3,1},{4,6},{5,7},{6,4},{7,5},{8,10},{9,11},{10,... | collective-permute-start | bytes 3080 | tf_op jit(solution)/shard_map/ppermute | solution.py:137
  7.3 3.2 %collective-permute-start.113 = (f32[8,128]{1,0:T(8,128)S(1)}, f32[8,128]{1,0:T(8,128)S(1)}, u32[]{:S(2)}, u32[]{:S(2)}) collective-permute-start(f32[8,128]{1,0:T(8,128)S(1)} %bitcast.54), channel_id=1, source_target_pairs={{4,0},{8,4},{12,8},{16,12},{20,16},{24,20},{28,24}} | collective-permute-start | bytes 12296 | tf_op jit(solution)/shard_map/ppermute | solution.py:424
  10.5 26.8 %copy-start = (bf16[256,256]{1,0:T(8,128)(2,1)S(1)}, bf16[256,256]{1,0:T(8,128)(2,1)}, u32[]{:S(2)}) copy-start(bf16[256,256]{1,0:T(8,128)(2,1)} %constant.17.clone.table_ref) | copy-start | bytes 393220
  10.5 26.8 %copy-start.1 = (s32[1,32]{1,0:T(1,128)S(1)}, s32[1,32]{1,0:T(1,128)}, u32[]{:S(2)}) copy-start(s32[1,32]{1,0:T(1,128)} %tag_ref.1) | copy-start | bytes 388
  12.5 17.8 %collective-permute-start.58 = (f32[161,8,128]{2,1,0:T(8,128)S(1)}, f32[161,8,128]{2,1,0:T(8,128)S(1)}, u32[]{:S(2)}, u32[]{:S(2)}) collective-permute-start(f32[161,8,128]{2,1,0:T(8,128)S(1)} %get-tuple-element.383), channel_id=1, source_target_pairs={{0,2},{1,3},{2,0},{3,1},{4,6},{5,7},{6,4},{7,5},{8,10},{9,11},{10,... | collective-permute-start | bytes 1978376 | tf_op jit(solution)/shard_map/cond/branch_19_fun/ppermute | solution.py:151
  12.7 10.6 %collective-permute-start.59 = (f32[34,8,128]{2,1,0:T(8,128)S(1)}, f32[34,8,128]{2,1,0:T(8,128)S(1)}, u32[]{:S(2)}, u32[]{:S(2)}) collective-permute-start(f32[34,8,128]{2,1,0:T(8,128)S(1)} %get-tuple-element.384), channel_id=1, source_target_pairs={{0,3},{1,0},{2,1},{3,2},{4,7},{5,4},{6,5},{7,6},{8,11},{9,8},{10,9... | collective-permute-start | bytes 417800 | tf_op jit(solution)/shard_map/cond/branch_19_fun/ppermute | solution.py:151
  14.2 9.0 %collective-permute-start.57 = (f32[33,8,128]{2,1,0:T(8,128)S(1)}, f32[33,8,128]{2,1,0:T(8,128)S(1)}, u32[]{:S(2)}, u32[]{:S(2)}) collective-permute-start(f32[33,8,128]{2,1,0:T(8,128)S(1)} %get-tuple-element.382), channel_id=1, source_target_pairs={{0,1},{1,2},{2,3},{3,0},{4,5},{5,6},{6,7},{7,4},{8,9},{9,10},{10,1... | collective-permute-start | bytes 405512 | tf_op jit(solution)/shard_map/cond/branch_19_fun/ppermute | solution.py:151
  32.3 4.9 %collective-permute-start.114 = (f32[8,128]{1,0:T(8,128)S(1)}, f32[8,128]{1,0:T(8,128)S(1)}, u32[]{:S(2)}, u32[]{:S(2)}) collective-permute-start(f32[8,128]{1,0:T(8,128)S(1)} %slice_bitcast_fusion), channel_id=1, source_target_pairs={{0,4},{4,8},{8,12},{12,16},{16,20},{20,24},{24,28}} | collective-permute-start | bytes 12296 | tf_op jit(solution)/shard_map/ppermute | solution.py:432

commit v2 on v1

--- a/solution.py
+++ b/solution.py
@@ -75,7 +75,7 @@
     return 1.0 + 0.5 * tag_ref[0, plan_ref[2, 1] + slot].astype(jnp.float32)
 
 
-def refine_kernel(plan_ref, tag_ref, held_ref, work_ref, ends_ref, before_ref, table_ref, out_ref, rows_ref):
+def refine_kernel(always, plan_ref, tag_ref, held_ref, work_ref, ends_ref, before_ref, after_ref, table_ref, out_ref, rows_ref):
     capacity, parts = held_ref.shape[:2]
     together, fine, wide = out_ref.shape
     edge, across = (fine // 2, wide // 4 // LANES)
@@ -94,13 +94,14 @@
 
         table = table_ref[...]
         lower = jnp.where(plan_ref[2, 4] == 0, ends_ref[0], before_ref[...])[:, None, :]
+        upper = after_ref[...] if always else jnp.where(plan_ref[2, 5] == 0, ends_ref[1], after_ref[...])
         for t in range(together):
             slot = base + t
             middle = part(slot, slice(None), slice(None))
             before = part(slot - 1, slice(parts - across, None), slice(SUBLANES - 1, None))
             after = part(slot + 1, slice(0, across), slice(0, 1))
             before = jnp.where(slot == 0, lower, before)
-            after = jnp.where(slot == live - 1, ends_ref[1][:, None, :], after)
+            after = jnp.where(slot == live - 1, upper[:, None, :], after)
             factor = tag_factor(plan_ref, tag_ref, jnp.minimum(slot, live - 1))
             if t:
                 middle, before, after = (jnp.where(slot < live, x, 0.0) for x in (middle, before, after))
@@ -111,15 +112,15 @@
             refined(flat(middle, across), flat(before, across), flat(after, across), factor, edge, table, rows_ref.at[t], put)
 
 
-def refine(held, work, plan, tags, ends, before, edge):
+def refine(held, work, plan, tags, ends, before, after, always, edge):
     capacity, parts = work.shape[:2]
     plane = parts * SUBLANES * LANES // edge
     table = window_table(edge)
     together = TOGETHER if capacity % TOGETHER == 0 else 1
     whole = lambda x: pl.BlockSpec(x.shape, lambda i, *_: (0,) * x.ndim)
-    operands = (held, work, ends, before, table)
+    operands = (held, work, ends, before, after, table)
     return pl.pallas_call(
-        refine_kernel,
+        functools.partial(refine_kernel, always),
         out_shape=jax.ShapeDtypeStruct((capacity, 2 * edge, 4 * plane), jnp.bfloat16),
         grid_spec=pltpu.PrefetchScalarGridSpec(
             num_scalar_prefetch=2,
@@ -139,6 +140,11 @@
 
 def all_of(rows, axis):
     count, bit = (lax.axis_size(axis), 1)
+    if count == 4:
+        others = []
+        for bits in (3, 1, 2):
+            others.append(swap(rows, axis, bits))
+        return jnp.concatenate([rows, others[1], others[2], others[0]], 0)
     while bit < count:
         other = swap(rows, axis, bit)
         rows = jnp.concatenate([rows, other], 0)
@@ -244,13 +250,13 @@
     offset = jnp.sum(jnp.where(lower, live, 0).astype(jnp.float32), axis=0, keepdims=True).astype(jnp.int32)
     kind = jnp.maximum(source, 0)
     index = jnp.where(kind > 0, rank, jnp.where(filled, place, 0))
-    values = [wide(live[:1]), wide(offset), wide(top_from[:1]), wide(top_place[:1]), start_flag]
+    values = [wide(live[:1]), wide(offset), wide(top_from[:1]), wide(top_place[:1]), start_flag, (wide(mine) == devices - 1).astype(jnp.int32)]
     sizes = values[0]
     for i, value in enumerate(values[1:], 1):
         sizes = jnp.where(lane == i, value, sizes)
     sent = jnp.where(lane == capacity, top_place, sent)
     table = jnp.where(row == 0, wide(kind[:1]), jnp.where(row == 1, wide(index[:1]), sizes))
-    plan_ref[...] = jnp.where(row > 2, behind(sent, 2), table)
+    plan_ref[...] = jnp.where(row > 2, behind(sent, 2), table)[:, : plan_ref.shape[1]]
 
 
 def make_plan(given, choices, capacity, steps):
@@ -258,7 +264,7 @@
     count = devices * max(1, SUBLANES // devices)
     return pl.pallas_call(
         functools.partial(plan_kernel, choices=choices, capacity=capacity, steps=steps),
-        out_shape=[jax.ShapeDtypeStruct((rows, LANES), jnp.int32) for rows in (count, 1)],
+        out_shape=[jax.ShapeDtypeStruct(shape, jnp.int32) for shape in ((count, 2 * SUBLANES), (1, LANES))],
         in_specs=[pl.BlockSpec(memory_space=pltpu.VMEM)],
         out_specs=[pl.BlockSpec(memory_space=pltpu.VMEM)] * 2,
         compiler_params=pltpu.CompilerParams(vmem_limit_bytes=1 << 20),
@@ -266,7 +272,7 @@
     )(given)
 
 
-def pack_kernel(sizes, last, plan_ref, patches_ref, after_ref, *refs):
+def pack_kernel(sizes, last, plan_ref, patches_ref, *refs):
     parcels, sems = refs[:-1], refs[-1]
     capacity, parts = patches_ref.shape[:2]
 
@@ -282,23 +288,14 @@
             act(pltpu.make_async_copy(last_plane(patches_ref, plan_ref[3 + k, capacity]), parcel.at[size * parts], sems.at[used]))
             used += 1
             if k == last:
-                upper = parcel.at[size * parts + 1]
-
-                @pl.when(plan_ref[2, 4] == 0)
-                def _():
-                    act(pltpu.make_async_copy(first_plane(patches_ref, 0), upper, sems.at[used]))
-
-                @pl.when(plan_ref[2, 4] != 0)
-                def _():
-                    act(pltpu.make_async_copy(after_ref, upper, sems.at[used]))
-
+                act(pltpu.make_async_copy(first_plane(patches_ref, 0), parcel.at[size * parts + 1], sems.at[used]))
                 used += 1
 
     each(lambda copy: copy.start())
     each(lambda copy: copy.wait())
 
 
-def pack(plan, patches, after, sizes, last):
+def pack(plan, patches, sizes, last):
     parts = patches.shape[1]
     return pl.pallas_call(
         functools.partial(pack_kernel, sizes, last),
@@ -309,13 +306,13 @@
         grid_spec=pltpu.PrefetchScalarGridSpec(
             num_scalar_prefetch=1,
             grid=(),
-            in_specs=[pl.BlockSpec(memory_space=pl.ANY)] * 2,
+            in_specs=[pl.BlockSpec(memory_space=pl.ANY)],
             out_specs=[pl.BlockSpec(memory_space=pl.ANY) for _ in sizes],
             scratch_shapes=[pltpu.SemaphoreType.DMA((sum(sizes) + len(sizes) + 1,))],
         ),
         compiler_params=pltpu.CompilerParams(vmem_limit_bytes=1 << 20),
         name="pack",
-    )(plan, patches, after)
+    )(plan, patches)
 
 
 def settle_kernel(plan_ref, patches_ref, held_ref, sems):
@@ -345,7 +342,7 @@
     )(plan, patches)
 
 
-def assemble_kernel(sizes, last, plan_ref, patches_ref, after_ref, *refs):
+def assemble_kernel(sizes, last, plan_ref, patches_ref, *refs):
     parcels, work_ref, ends_ref, sems = refs[:-3], refs[-3], refs[-2], refs[-1]
     capacity, parts = work_ref.shape[:2]
 
@@ -363,7 +360,8 @@
     def _():
         put(last_plane(patches_ref, slot), 0)
 
-    put(after_ref if last is None else parcels[last].at[sizes[last] * parts + 1], 1)
+    put(first_plane(patches_ref, 0) if last is None else parcels[last].at[sizes[last] * parts + 1], 1)
+    put(first_plane(patches_ref, 0), 2)
 
     @pl.loop(0, capacity)
     def _(j):
@@ -373,7 +371,7 @@
             def _(parcel=parcel):
                 pltpu.make_async_copy(parcel.at[pl.ds(plan_ref[1, j] * parts, parts)], work_ref.at[j], sems.at[j]).start()
 
-    for side in (0, 1):
+    for side in range(3):
         pltpu.make_async_copy(patches_ref.at[0, 0], ends_ref.at[side], sems.at[capacity + side]).wait()
 
     @pl.loop(0, capacity)
@@ -383,29 +381,29 @@
             pltpu.make_async_copy(patches_ref.at[0], work_ref.at[j], sems.at[j]).wait()
 
 
-def assemble(plan, patches, after, arrived, sizes, last):
+def assemble(plan, patches, arrived, sizes, last):
     return pl.pallas_call(
         functools.partial(assemble_kernel, sizes, last),
         out_shape=[
             jax.ShapeDtypeStruct(patches.shape, patches.dtype),
-            jax.ShapeDtypeStruct((2,) + patches.shape[2:], patches.dtype),
+            jax.ShapeDtypeStruct((3,) + patches.shape[2:], patches.dtype),
         ],
         grid_spec=pltpu.PrefetchScalarGridSpec(
             num_scalar_prefetch=1,
             grid=(),
-            in_specs=[pl.BlockSpec(memory_space=pl.ANY) for _ in range(2 + len(arrived))],
+            in_specs=[pl.BlockSpec(memory_space=pl.ANY) for _ in range(1 + len(arrived))],
             out_specs=[pl.BlockSpec(memory_space=pl.ANY)] * 2,
-            scratch_shapes=[pltpu.SemaphoreType.DMA((patches.shape[0] + 2,))],
+            scratch_shapes=[pltpu.SemaphoreType.DMA((patches.shape[0] + 3,))],
         ),
         compiler_params=pltpu.CompilerParams(vmem_limit_bytes=1 << 20),
         name="assemble",
-    )(plan, patches, after, *arrived)
-
-
-def exchange(sizes, last, plan, patches, after):
-    parcels = pack(plan, patches, after, sizes, last)
+    )(plan, patches, *arrived)
+
+
+def exchange(sizes, last, plan, patches):
+    parcels = pack(plan, patches, sizes, last)
     arrived = [forward(parcel, "blk", 1 + k) for k, parcel in enumerate(parcels)]
-    return settle(plan, patches), *assemble(plan, patches, after, arrived, sizes, last)
+    return settle(plan, patches), *assemble(plan, patches, arrived, sizes, last)
 
 
 def body(patches, counts, moves, tags):
@@ -417,20 +415,16 @@
     mine = lax.axis_index("blk").astype(jnp.int32).reshape(1, 1)
     row = jnp.pad(jnp.concatenate([counts[:, None], moves, mine], 1), ((0, 0), (0, LANES - steps - 2)))
     given = all_of(lax.optimization_barrier(row), "blk")
-    first = parts[0, :SUBLANES, 0]
     line = ("grp", "blk")
-    if parcels == devices - 1:
-        last = parcels - 1
-        after = lax.ppermute(first, line, [((g + 1) * devices, g * devices) for g in range(groups - 1)])
-    else:
-        last = None
-        after = lax.ppermute(first, line, [(i + 1, i) for i in range(groups * devices - 1)])
+    last = parcels - 1 if parcels == devices - 1 else None
     plan, picks = make_plan(given, choices, capacity, steps)
     pick = jnp.minimum(picks[0, 0], lax.axis_index("grp") + len(choices))
     branches = [functools.partial(exchange, choice + (0,) * (parcels - len(choice)), last) for choice in choices]
-    held, work, ends = lax.switch(pick, branches, plan, parts, after)
+    held, work, ends = lax.switch(pick, branches, plan, parts)
     before = lax.ppermute(ends[0], line, [(g * devices, (g + 1) * devices) for g in range(groups - 1)])
-    return refine(held, work, plan, tags, ends, before, edge)
+    stride = 1 if last is None else devices
+    after = lax.ppermute(ends[2], line, [(i, i - 1) for i in range(stride, groups * devices, stride)])
+    return refine(held, work, plan, tags, ends, before, after, last is None, edge)
 
 
 def solution(mesh):

time: 42.3 us -> 38.8 us (0.917)
  the two profiles are of different devices: /device:TPU:16 before, /device:TPU:24 now
where the time goes in v2:
time: 38.8 us; the launch traced here: 38.6 us
  waiting for transfers between devices  13.8 us (36%)
  starting transfers between devices  12.5 us (32%)
  Pallas kernels  10.5 us (27%)
  between operations  0.77 us (2%)
  other arithmetic  0.74 us (2%)
    ppermute x3, waiting for transfers between devices, forward(): lax.ppermute(block, axis, [(i, (i + distance) % count) for i in range(cou...  6.54 us
    pallas_call x1, Pallas kernels, refine(): pl.pallas_call(functools.partial(refine_kernel, always), out_shape=jax.Sh...  4.53 us
    ppermute x1, waiting for transfers between devices, body(): lax.ppermute(ends[0], line, [(g * devices, (g + 1) * devices) for g in ra...  4.19 us
    ppermute x1, starting transfers between devices, body(): lax.ppermute(ends[0], line, [(g * devices, (g + 1) * devices) for g in ra...  4 us
    ppermute x3, starting transfers between devices, forward(): lax.ppermute(block, axis, [(i, (i + distance) % count) for i in range(cou...  3.6 us
    ppermute x3, starting transfers between devices, swap(): lax.ppermute(block, axis, [(i, i ^ bit) for i in range(lax.axis_size(axis...  3.5 us
    ppermute x3, waiting for transfers between devices, swap(): lax.ppermute(block, axis, [(i, i ^ bit) for i in range(lax.axis_size(axis...  3.03 us
    pallas_call x1, Pallas kernels, settle(): pl.pallas_call(settle_kernel, out_shape=jax.ShapeDtypeStruct(patches.shap...  2.1 us
  transfers between devices with their start and end apart: 8, of which 6 were waited for; matrix products, arithmetic and copies ran while one was open for 0% of the time, Pallas kernels for 5%

profile of v2, /device:TPU:24, one launch (start us, length us, event | category | flops | bytes accessed | tf_op | source)
XLA Modules:
  0.0 38.6 jit_solution(10530665033732093462)
XLA Ops:
  0.7 0.7 %pad_add_fusion.1 = s32[1,6]{1,0:T(1,128)S(1)} fusion(s32[1,1]{1,0:T(1,128)} %bitcast.1, s32[1,4]{1,0:T(1,128)} %param.44, s32[1,1]{1,0:T(1,128)} %bitcast.13), kind=kLoop, calls=%fused_computation.3 | loop fusion | flops 12 | bytes 48 | tf_op jit(solution)/shard_map/concatenate | solution.py:416
  1.4 2.5 %collective-permute-start.113 = (s32[1,128]{1,0:T(1,128)S(1)}, s32[1,128]{1,0:T(1,128)S(1)}, u32[]{:S(2)}, u32[]{:S(2)}) collective-permute-start(s32[1,128]{1,0:T(1,128)S(1)} %pad.4), channel_id=1, source_target_pairs={{0,3},{1,2},{2,1},{3,0},{4,7},{5,6},{6,5},{7,4},{8,11},{9,10},{10,... | collective-permute-start | bytes 1544 | tf_op jit(solution)/shard_map/ppermute | solution.py:138
  3.9 0.5 %collective-permute-start.112 = (s32[1,128]{1,0:T(1,128)S(1)}, s32[1,128]{1,0:T(1,128)S(1)}, u32[]{:S(2)}, u32[]{:S(2)}) collective-permute-start(s32[1,128]{1,0:T(1,128)S(1)} %pad.4), channel_id=1, source_target_pairs={{0,2},{1,3},{2,0},{3,1},{4,6},{5,7},{6,4},{7,5},{8,10},{9,11},{10,... | collective-permute-start | bytes 1544 | tf_op jit(solution)/shard_map/ppermute | solution.py:138
  4.4 0.5 %collective-permute-start.111 = (s32[1,128]{1,0:T(1,128)S(1)}, s32[1,128]{1,0:T(1,128)S(1)}, u32[]{:S(2)}, u32[]{:S(2)}) collective-permute-start(s32[1,128]{1,0:T(1,128)S(1)} %pad.4), channel_id=1, source_target_pairs={{0,1},{1,0},{2,3},{3,2},{4,5},{5,4},{6,7},{7,6},{8,9},{9,8},{10,11... | collective-permute-start | bytes 1544 | tf_op jit(solution)/shard_map/ppermute | solution.py:138
  4.9 1.0 %collective-permute-done.113 = s32[1,128]{1,0:T(1,128)S(1)} collective-permute-done((s32[1,128]{1,0:T(1,128)S(1)}, s32[1,128]{1,0:T(1,128)S(1)}, u32[]{:S(2)}, u32[]{:S(2)}) %collective-permute-start.113) | collective-permute-done | bytes 544 | tf_op jit(solution)/shard_map/ppermute | solution.py:138
  5.9 1.5 %collective-permute-done.112 = s32[1,128]{1,0:T(1,128)S(1)} collective-permute-done((s32[1,128]{1,0:T(1,128)S(1)}, s32[1,128]{1,0:T(1,128)S(1)}, u32[]{:S(2)}, u32[]{:S(2)}) %collective-permute-start.112) | collective-permute-done | bytes 544 | tf_op jit(solution)/shard_map/ppermute | solution.py:138
  7.4 0.5 %collective-permute-done.111 = s32[1,128]{1,0:T(1,128)S(1)} collective-permute-done((s32[1,128]{1,0:T(1,128)S(1)}, s32[1,128]{1,0:T(1,128)S(1)}, u32[]{:S(2)}, u32[]{:S(2)}) %collective-permute-start.111) | collective-permute-done | bytes 544 | tf_op jit(solution)/shard_map/ppermute | solution.py:138
  7.9 0.4 %plan.1 = (s32[8,16]{1,0:T(8,128)S(1)}, s32[1,128]{1,0:T(1,128)S(1)}) custom-call(s32[4,128]{1,0:T(4,128)S(1)} %pad_add_fusion.given_ref), custom_call_target="tpu_custom_call" | custom-call | tf_op jit(solution)/shard_map/plan/pallas_call | solution.py:265
  8.4 0.0 copy-start
  8.4 0.0 copy-start.1
  8.4 16.0 %conditional.1 = (f32[8,32,8,128]{3,2,1,0:T(8,128)S(1)}, f32[8,32,8,128]{3,2,1,0:T(8,128)S(1)}, f32[3,8,128]{2,1,0:T(8,128)S(1)}) conditional(s32[]{:T(128)} %clamp.3, (s32[8,16]{1,0:T(8,128)S(1)}, f32[8,32,8,128]{3,2,1,0:T(8,128)}) %tuple.210, (s32[8,16]{1,0:T(8,128)S(1)}, f32[8,32,8,128]{3,2,1,0:T(8,128)}) %tuple.228, ...), branch_computations={%region_0.1_spmd, %region_1.2_spmd, %region_2.3_spmd, %region_3.4_... | conditional | flops 16777216 | bytes 13172880 | solution.py:423
  8.5 1.9 %pack.42 = (f32[33,8,128]{2,1,0:T(8,128)S(1)}, f32[65,8,128]{2,1,0:T(8,128)S(1)}, f32[66,8,128]{2,1,0:T(8,128)S(1)}) custom-call(s32[8,16]{1,0:T(8,128)S(1)} %get-tuple-element.188.plan_ref, f32[8,32,8,128]{3,2,1,0:T(8,128)} %get-tuple-element.189.patches_ref), custom_call_target="tpu_custom_call" | custom-call | tf_op jit(solution)/shard_map/cond/branch_5_fun/pack/pallas_call | solution.py:300
  10.4 1.6 %collective-permute-start.17 = (f32[66,8,128]{2,1,0:T(8,128)S(1)}, f32[66,8,128]{2,1,0:T(8,128)S(1)}, u32[]{:S(2)}, u32[]{:S(2)}) collective-permute-start(f32[66,8,128]{2,1,0:T(8,128)S(1)} %get-tuple-element.192), channel_id=1, source_target_pairs={{0,3},{1,0},{2,1},{3,2},{4,7},{5,4},{6,5},{7,6},{8,11},{9,8},{10,9... | collective-permute-start | bytes 811016 | tf_op jit(solution)/shard_map/cond/branch_5_fun/ppermute | solution.py:157
  11.9 0.5 %collective-permute-start.16 = (f32[65,8,128]{2,1,0:T(8,128)S(1)}, f32[65,8,128]{2,1,0:T(8,128)S(1)}, u32[]{:S(2)}, u32[]{:S(2)}) collective-permute-start(f32[65,8,128]{2,1,0:T(8,128)S(1)} %get-tuple-element.191), channel_id=1, source_target_pairs={{0,2},{1,3},{2,0},{3,1},{4,6},{5,7},{6,4},{7,5},{8,10},{9,11},{10,... | collective-permute-start | bytes 798728 | tf_op jit(solution)/shard_map/cond/branch_5_fun/ppermute | solution.py:157
  12.4 1.5 %collective-permute-start.15 = (f32[33,8,128]{2,1,0:T(8,128)S(1)}, f32[33,8,128]{2,1,0:T(8,128)S(1)}, u32[]{:S(2)}, u32[]{:S(2)}) collective-permute-start(f32[33,8,128]{2,1,0:T(8,128)S(1)} %get-tuple-element.190), channel_id=1, source_target_pairs={{0,1},{1,2},{2,3},{3,0},{4,5},{5,6},{6,7},{7,4},{8,9},{9,10},{10,1... | collective-permute-start | bytes 405512 | tf_op jit(solution)/shard_map/cond/branch_5_fun/ppermute | solution.py:157
  14.0 2.1 %settle.42 = f32[8,32,8,128]{3,2,1,0:T(8,128)S(1)} custom-call(s32[8,16]{1,0:T(8,128)S(1)} %get-tuple-element.188.plan_ref, f32[8,32,8,128]{3,2,1,0:T(8,128)} %get-tuple-element.189.patches_ref), custom_call_target="tpu_custom_call" | custom-call | flops 16777216 | bytes 2097152 | tf_op jit(solution)/shard_map/cond/branch_5_fun/settle/pallas_call | solution.py:329
  16.1 6.1 %collective-permute-done.15.refs_0_ = f32[33,8,128]{2,1,0:T(8,128)S(1)} collective-permute-done((f32[33,8,128]{2,1,0:T(8,128)S(1)}, f32[33,8,128]{2,1,0:T(8,128)S(1)}, u32[]{:S(2)}, u32[]{:S(2)}) %collective-permute-start.15) | collective-permute-done | bytes 135200 | tf_op jit(solution)/shard_map/cond/branch_5_fun/ppermute | solution.py:157
  22.2 0.4 %collective-permute-done.16.refs_1_ = f32[65,8,128]{2,1,0:T(8,128)S(1)} collective-permute-done((f32[65,8,128]{2,1,0:T(8,128)S(1)}, f32[65,8,128]{2,1,0:T(8,128)S(1)}, u32[]{:S(2)}, u32[]{:S(2)}) %collective-permute-start.16) | collective-permute-done | bytes 266272 | tf_op jit(solution)/shard_map/cond/branch_5_fun/ppermute | solution.py:157
  22.6 0.0 collective-permute-done.17.refs_2_
  22.6 1.6 %assemble.42 = (f32[8,32,8,128]{3,2,1,0:T(8,128)S(1)}, f32[3,8,128]{2,1,0:T(8,128)S(1)}) custom-call(s32[8,16]{1,0:T(8,128)S(1)} %get-tuple-element.188.plan_ref, f32[8,32,8,128]{3,2,1,0:T(8,128)} %get-tuple-element.189.patches_ref, f32[33,8,128]{2,1,0:T(8,128)S(1)} %collective-permute-done.15.refs_0_, f32[65,8,128]{2,1,0:T(8,128)S(1)} %collective-permute-done.16.refs_1_, ...), custom_call_target="tpu_custom_call" | custom-call | tf_op jit(solution)/shard_map/cond/branch_5_fun/assemble/pallas_call | solution.py:385
  24.5 1.4 %collective-permute-start.115 = (f32[8,128]{1,0:T(8,128)S(1)}, f32[8,128]{1,0:T(8,128)S(1)}, u32[]{:S(2)}, u32[]{:S(2)}) collective-permute-start(f32[8,128]{1,0:T(8,128)S(1)} %get-tuple-element.422), channel_id=1, source_target_pairs={{4,3},{8,7},{12,11},{16,15},{20,19},{24,23},{28,27}} | collective-permute-start | bytes 12296 | tf_op jit(solution)/shard_map/ppermute | solution.py:426
  25.9 4.0 %collective-permute-start.114 = (f32[8,128]{1,0:T(8,128)S(1)}, f32[8,128]{1,0:T(8,128)S(1)}, u32[]{:S(2)}, u32[]{:S(2)}) collective-permute-start(f32[8,128]{1,0:T(8,128)S(1)} %get-tuple-element.423), channel_id=1, source_target_pairs={{0,4},{4,8},{8,12},{12,16},{16,20},{20,24},{24,28}} | collective-permute-start | bytes 12296 | tf_op jit(solution)/shard_map/ppermute | solution.py:424
  29.9 0.0 collective-permute-done.115.after_ref
  29.9 4.2 %collective-permute-done.114.before_ref = f32[8,128]{1,0:T(8,128)S(1)} collective-permute-done((f32[8,128]{1,0:T(8,128)S(1)}, f32[8,128]{1,0:T(8,128)S(1)}, u32[]{:S(2)}, u32[]{:S(2)}) %collective-permute-start.114) | collective-permute-done | bytes 4128 | tf_op jit(solution)/shard_map/ppermute | solution.py:424
  34.1 0.0 copy-done
  34.1 0.0 copy-done.1
  34.1 4.5 %refine.1 = bf16[8,64,4096]{2,1,0:T(8,128)(2,1)} custom-call(s32[8,16]{1,0:T(8,128)S(1)} %get-tuple-element.417.plan_ref, s32[1,32]{1,0:T(1,128)S(1)} %copy-done.1, f32[8,32,8,128]{3,2,1,0:T(8,128)S(1)} %get-tuple-element.419.held_ref, f32[8,32,8,128]{3,2,1,0:T(8,128)S(1)} %get-tuple-element.420.work_ref, f32[3,8,128]{2,1,0:T(8,128)S(1)} %get-tuple-element.421.ends_ref, ...), custom_call_target="tpu_custom_call" | custom-call | tf_op jit(solution)/shard_map/refine/pallas_call | solution.py:122
  (3 shorter events, 0.0 us)
Async XLA Ops:
  1.4 4.5 %collective-permute-start.113 = (s32[1,128]{1,0:T(1,128)S(1)}, s32[1,128]{1,0:T(1,128)S(1)}, u32[]{:S(2)}, u32[]{:S(2)}) collective-permute-start(s32[1,128]{1,0:T(1,128)S(1)} %pad.4), channel_id=1, source_target_pairs={{0,3},{1,2},{2,1},{3,0},{4,7},{5,6},{6,5},{7,4},{8,11},{9,10},{10,... | collective-permute-start | bytes 1544 | tf_op jit(solution)/shard_map/ppermute | solution.py:138
  3.9 3.6 %collective-permute-start.112 = (s32[1,128]{1,0:T(1,128)S(1)}, s32[1,128]{1,0:T(1,128)S(1)}, u32[]{:S(2)}, u32[]{:S(2)}) collective-permute-start(s32[1,128]{1,0:T(1,128)S(1)} %pad.4), channel_id=1, source_target_pairs={{0,2},{1,3},{2,0},{3,1},{4,6},{5,7},{6,4},{7,5},{8,10},{9,11},{10,... | collective-permute-start | bytes 1544 | tf_op jit(solution)/shard_map/ppermute | solution.py:138
  4.4 3.6 %collective-permute-start.111 = (s32[1,128]{1,0:T(1,128)S(1)}, s32[1,128]{1,0:T(1,128)S(1)}, u32[]{:S(2)}, u32[]{:S(2)}) collective-permute-start(s32[1,128]{1,0:T(1,128)S(1)} %pad.4), channel_id=1, source_target_pairs={{0,1},{1,0},{2,3},{3,2},{4,5},{5,4},{6,7},{7,6},{8,9},{9,8},{10,11... | collective-permute-start | bytes 1544 | tf_op jit(solution)/shard_map/ppermute | solution.py:138
  8.4 25.7 %copy-start = (bf16[256,256]{1,0:T(8,128)(2,1)S(1)}, bf16[256,256]{1,0:T(8,128)(2,1)}, u32[]{:S(2)}) copy-start(bf16[256,256]{1,0:T(8,128)(2,1)} %constant.17.clone.table_ref) | copy-start | bytes 393220
  8.4 25.7 %copy-start.1 = (s32[1,32]{1,0:T(1,128)S(1)}, s32[1,32]{1,0:T(1,128)}, u32[]{:S(2)}) copy-start(s32[1,32]{1,0:T(1,128)} %tag_ref.1) | copy-start | bytes 388
  10.4 12.3 %collective-permute-start.17 = (f32[66,8,128]{2,1,0:T(8,128)S(1)}, f32[66,8,128]{2,1,0:T(8,128)S(1)}, u32[]{:S(2)}, u32[]{:S(2)}) collective-permute-start(f32[66,8,128]{2,1,0:T(8,128)S(1)} %get-tuple-element.192), channel_id=1, source_target_pairs={{0,3},{1,0},{2,1},{3,2},{4,7},{5,4},{6,5},{7,6},{8,11},{9,8},{10,9... | collective-permute-start | bytes 811016 | tf_op jit(solution)/shard_map/cond/branch_5_fun/ppermute | solution.py:157
  11.9 10.7 %collective-permute-start.16 = (f32[65,8,128]{2,1,0:T(8,128)S(1)}, f32[65,8,128]{2,1,0:T(8,128)S(1)}, u32[]{:S(2)}, u32[]{:S(2)}) collective-permute-start(f32[65,8,128]{2,1,0:T(8,128)S(1)} %get-tuple-element.191), channel_id=1, source_target_pairs={{0,2},{1,3},{2,0},{3,1},{4,6},{5,7},{6,4},{7,5},{8,10},{9,11},{10,... | collective-permute-start | bytes 798728 | tf_op jit(solution)/shard_map/cond/branch_5_fun/ppermute | solution.py:157
  12.4 9.8 %collective-permute-start.15 = (f32[33,8,128]{2,1,0:T(8,128)S(1)}, f32[33,8,128]{2,1,0:T(8,128)S(1)}, u32[]{:S(2)}, u32[]{:S(2)}) collective-permute-start(f32[33,8,128]{2,1,0:T(8,128)S(1)} %get-tuple-element.190), channel_id=1, source_target_pairs={{0,1},{1,2},{2,3},{3,0},{4,5},{5,6},{6,7},{7,4},{8,9},{9,10},{10,1... | collective-permute-start | bytes 405512 | tf_op jit(solution)/shard_map/cond/branch_5_fun/ppermute | solution.py:157
  24.5 5.4 %collective-permute-start.115 = (f32[8,128]{1,0:T(8,128)S(1)}, f32[8,128]{1,0:T(8,128)S(1)}, u32[]{:S(2)}, u32[]{:S(2)}) collective-permute-start(f32[8,128]{1,0:T(8,128)S(1)} %get-tuple-element.422), channel_id=1, source_target_pairs={{4,3},{8,7},{12,11},{16,15},{20,19},{24,23},{28,27}} | collective-permute-start | bytes 12296 | tf_op jit(solution)/shard_map/ppermute | solution.py:426
  25.9 8.2 %collective-permute-start.114 = (f32[8,128]{1,0:T(8,128)S(1)}, f32[8,128]{1,0:T(8,128)S(1)}, u32[]{:S(2)}, u32[]{:S(2)}) collective-permute-start(f32[8,128]{1,0:T(8,128)S(1)} %get-tuple-element.423), channel_id=1, source_target_pairs={{0,4},{4,8},{8,12},{12,16},{16,20},{20,24},{24,28}} | collective-permute-start | bytes 12296 | tf_op jit(solution)/shard_map/ppermute | solution.py:424

commit v3 on v2

--- a/solution.py
+++ b/solution.py
@@ -14,10 +14,12 @@
 SUBLANES = 8
 TOGETHER = 2
 CHOICES = (
-    (4, 3, 3), (5, 4, 4), (3, 2, 2), (2, 4, 2), (2, 2, 2), (3, 5, 3), (3, 3, 3), (5, 2, 2), (4, 2, 2),
-    (2, 3, 2), (2, 2, 3), (4, 1, 1), (1, 3, 1), (1, 1, 2), (3, 1, 1), (5, 1, 1), (1, 2, 1), (2, 2, 4),
-    (6, 1, 1), (2, 1, 1), (2, 5, 2), (1, 1, 3), (1, 4, 1), (3, 4, 1), (3, 3, 1), (5, 3, 3), (1, 1, 1),
-    (3, 2, 1), (1, 5, 1), (2, 2, 1), (2, 3, 1), (3, 1, 2), (4, 3, 1), (2, 1, 2), (4, 2, 1), (1, 2, 2),
+    (0, 2, 3), (1, 1, 1), (1, 1, 2), (1, 1, 3), (1, 2, 1), (1, 2, 2), (1, 3, 1), (1, 3, 2), (1, 3, 3),
+    (1, 4, 1), (1, 5, 1), (2, 1, 1), (2, 1, 2), (2, 1, 3), (2, 2, 1), (2, 2, 2), (2, 2, 3), (2, 2, 4),
+    (2, 3, 1), (2, 3, 2), (2, 4, 1), (2, 4, 2), (2, 5, 2), (3, 1, 1), (3, 1, 2), (3, 1, 3), (3, 2, 1),
+    (3, 2, 2), (3, 3, 0), (3, 3, 1), (3, 3, 3), (3, 4, 1), (3, 5, 3), (4, 1, 1), (4, 1, 2), (4, 1, 3),
+    (4, 2, 1), (4, 2, 2), (4, 3, 1), (4, 3, 3), (5, 1, 1), (5, 1, 2), (5, 2, 1), (5, 2, 2), (5, 3, 0),
+    (5, 3, 3), (5, 4, 4), (6, 1, 1), (6, 5, 4),
 )
 
 
@@ -164,7 +166,7 @@
     else:
         choices = {(u,) * distances for u in (1, 2, 3, 4)}
     choices = {tuple(min(c, most) for c in choice) for choice in choices} | {(most,) * distances}
-    load = lambda c: (max(a + b for a, b in itertools.combinations(c + (0, 0), 2)), sum(c), c)
+    load = lambda c: (max(a + b for a, b in itertools.combinations(c + (0, 0), 2)) + 0.05 * sum(c), c)
     return sorted(choices, key=load)
 
 

time: 38.8 us -> 38.6 us (level)
  no operation moved by 1% of the time
where the time goes in v3:
time: 38.6 us; the launch traced here: 38.4 us
  waiting for transfers between devices  13.6 us (35%)
  starting transfers between devices  12.5 us (32%)
  Pallas kernels  10.5 us (27%)
  between operations  0.77 us (2%)
  other arithmetic  0.74 us (2%)
    ppermute x3, waiting for transfers between devices, forward(): lax.ppermute(block, axis, [(i, (i + distance) % count) for i in range(cou...  6.52 us
    pallas_call x1, Pallas kernels, refine(): pl.pallas_call(functools.partial(refine_kernel, always), out_shape=jax.Sh...  4.53 us
    ppermute x1, starting transfers between devices, body(): lax.ppermute(ends[0], line, [(g * devices, (g + 1) * devices) for g in ra...  4.03 us
    ppermute x1, waiting for transfers between devices, body(): lax.ppermute(ends[0], line, [(g * devices, (g + 1) * devices) for g in ra...  4 us
    ppermute x3, starting transfers between devices, forward(): lax.ppermute(block, axis, [(i, (i + distance) % count) for i in range(cou...  3.6 us
    ppermute x3, starting transfers between devices, swap(): lax.ppermute(block, axis, [(i, i ^ bit) for i in range(lax.axis_size(axis...  3.5 us
    ppermute x3, waiting for transfers between devices, swap(): lax.ppermute(block, axis, [(i, i ^ bit) for i in range(lax.axis_size(axis...  3.03 us
    pallas_call x1, Pallas kernels, settle(): pl.pallas_call(settle_kernel, out_shape=jax.ShapeDtypeStruct(patches.shap...  2.1 us
  transfers between devices with their start and end apart: 8, of which 6 were waited for; matrix products, arithmetic and copies ran while one was open for 0% of the time, Pallas kernels for 5%

profile of v3, /device:TPU:24, one launch (start us, length us, event | category | flops | bytes accessed | tf_op | source)
XLA Modules:
  0.0 38.4 jit_solution(3969778943398057233)
XLA Ops:
  0.7 0.7 %pad_add_fusion.1 = s32[1,6]{1,0:T(1,128)S(1)} fusion(s32[1,1]{1,0:T(1,128)} %bitcast.1, s32[1,4]{1,0:T(1,128)} %param.57, s32[1,1]{1,0:T(1,128)} %bitcast.13), kind=kLoop, calls=%fused_computation.3 | loop fusion | flops 12 | bytes 48 | tf_op jit(solution)/shard_map/concatenate | solution.py:418
  1.4 2.5 %collective-permute-start.152 = (s32[1,128]{1,0:T(1,128)S(1)}, s32[1,128]{1,0:T(1,128)S(1)}, u32[]{:S(2)}, u32[]{:S(2)}) collective-permute-start(s32[1,128]{1,0:T(1,128)S(1)} %pad.4), channel_id=1, source_target_pairs={{0,3},{1,2},{2,1},{3,0},{4,7},{5,6},{6,5},{7,4},{8,11},{9,10},{10,... | collective-permute-start | bytes 1544 | tf_op jit(solution)/shard_map/ppermute | solution.py:140
  3.9 0.5 %collective-permute-start.151 = (s32[1,128]{1,0:T(1,128)S(1)}, s32[1,128]{1,0:T(1,128)S(1)}, u32[]{:S(2)}, u32[]{:S(2)}) collective-permute-start(s32[1,128]{1,0:T(1,128)S(1)} %pad.4), channel_id=1, source_target_pairs={{0,2},{1,3},{2,0},{3,1},{4,6},{5,7},{6,4},{7,5},{8,10},{9,11},{10,... | collective-permute-start | bytes 1544 | tf_op jit(solution)/shard_map/ppermute | solution.py:140
  4.4 0.5 %collective-permute-start.150 = (s32[1,128]{1,0:T(1,128)S(1)}, s32[1,128]{1,0:T(1,128)S(1)}, u32[]{:S(2)}, u32[]{:S(2)}) collective-permute-start(s32[1,128]{1,0:T(1,128)S(1)} %pad.4), channel_id=1, source_target_pairs={{0,1},{1,0},{2,3},{3,2},{4,5},{5,4},{6,7},{7,6},{8,9},{9,8},{10,11... | collective-permute-start | bytes 1544 | tf_op jit(solution)/shard_map/ppermute | solution.py:140
  4.9 1.0 %collective-permute-done.152 = s32[1,128]{1,0:T(1,128)S(1)} collective-permute-done((s32[1,128]{1,0:T(1,128)S(1)}, s32[1,128]{1,0:T(1,128)S(1)}, u32[]{:S(2)}, u32[]{:S(2)}) %collective-permute-start.152) | collective-permute-done | bytes 544 | tf_op jit(solution)/shard_map/ppermute | solution.py:140
  5.9 1.5 %collective-permute-done.151 = s32[1,128]{1,0:T(1,128)S(1)} collective-permute-done((s32[1,128]{1,0:T(1,128)S(1)}, s32[1,128]{1,0:T(1,128)S(1)}, u32[]{:S(2)}, u32[]{:S(2)}) %collective-permute-start.151) | collective-permute-done | bytes 544 | tf_op jit(solution)/shard_map/ppermute | solution.py:140
  7.4 0.5 %collective-permute-done.150 = s32[1,128]{1,0:T(1,128)S(1)} collective-permute-done((s32[1,128]{1,0:T(1,128)S(1)}, s32[1,128]{1,0:T(1,128)S(1)}, u32[]{:S(2)}, u32[]{:S(2)}) %collective-permute-start.150) | collective-permute-done | bytes 544 | tf_op jit(solution)/shard_map/ppermute | solution.py:140
  7.9 0.4 %plan.1 = (s32[8,16]{1,0:T(8,128)S(1)}, s32[1,128]{1,0:T(1,128)S(1)}) custom-call(s32[4,128]{1,0:T(4,128)S(1)} %pad_add_fusion.given_ref), custom_call_target="tpu_custom_call" | custom-call | tf_op jit(solution)/shard_map/plan/pallas_call | solution.py:267
  8.4 0.0 copy-start
  8.4 0.0 copy-start.1
  8.4 16.0 %conditional.1 = (f32[8,32,8,128]{3,2,1,0:T(8,128)S(1)}, f32[8,32,8,128]{3,2,1,0:T(8,128)S(1)}, f32[3,8,128]{2,1,0:T(8,128)S(1)}) conditional(s32[]{:T(128)} %clamp.3, (s32[8,16]{1,0:T(8,128)S(1)}, f32[8,32,8,128]{3,2,1,0:T(8,128)}) %tuple.281, (s32[8,16]{1,0:T(8,128)S(1)}, f32[8,32,8,128]{3,2,1,0:T(8,128)}) %tuple.306, ...), branch_computations={%region_0.1_spmd, %region_1.2_spmd, %region_2.3_spmd, %region_3.4_... | conditional | flops 16777216 | bytes 13172880 | solution.py:425
  8.5 1.9 %pack.55 = (f32[33,8,128]{2,1,0:T(8,128)S(1)}, f32[65,8,128]{2,1,0:T(8,128)S(1)}, f32[66,8,128]{2,1,0:T(8,128)S(1)}) custom-call(s32[8,16]{1,0:T(8,128)S(1)} %get-tuple-element.240.plan_ref, f32[8,32,8,128]{3,2,1,0:T(8,128)} %get-tuple-element.241.patches_ref), custom_call_target="tpu_custom_call" | custom-call | tf_op jit(solution)/shard_map/cond/branch_5_fun/pack/pallas_call | solution.py:302
  10.4 1.6 %collective-permute-start.17 = (f32[66,8,128]{2,1,0:T(8,128)S(1)}, f32[66,8,128]{2,1,0:T(8,128)S(1)}, u32[]{:S(2)}, u32[]{:S(2)}) collective-permute-start(f32[66,8,128]{2,1,0:T(8,128)S(1)} %get-tuple-element.244), channel_id=1, source_target_pairs={{0,3},{1,0},{2,1},{3,2},{4,7},{5,4},{6,5},{7,6},{8,11},{9,8},{10,9... | collective-permute-start | bytes 811016 | tf_op jit(solution)/shard_map/cond/branch_5_fun/ppermute | solution.py:159
  11.9 0.5 %collective-permute-start.16 = (f32[65,8,128]{2,1,0:T(8,128)S(1)}, f32[65,8,128]{2,1,0:T(8,128)S(1)}, u32[]{:S(2)}, u32[]{:S(2)}) collective-permute-start(f32[65,8,128]{2,1,0:T(8,128)S(1)} %get-tuple-element.243), channel_id=1, source_target_pairs={{0,2},{1,3},{2,0},{3,1},{4,6},{5,7},{6,4},{7,5},{8,10},{9,11},{10,... | collective-permute-start | bytes 798728 | tf_op jit(solution)/shard_map/cond/branch_5_fun/ppermute | solution.py:159
  12.4 1.5 %collective-permute-start.15 = (f32[33,8,128]{2,1,0:T(8,128)S(1)}, f32[33,8,128]{2,1,0:T(8,128)S(1)}, u32[]{:S(2)}, u32[]{:S(2)}) collective-permute-start(f32[33,8,128]{2,1,0:T(8,128)S(1)} %get-tuple-element.242), channel_id=1, source_target_pairs={{0,1},{1,2},{2,3},{3,0},{4,5},{5,6},{6,7},{7,4},{8,9},{9,10},{10,1... | collective-permute-start | bytes 405512 | tf_op jit(solution)/shard_map/cond/branch_5_fun/ppermute | solution.py:159
  14.0 2.1 %settle.55 = f32[8,32,8,128]{3,2,1,0:T(8,128)S(1)} custom-call(s32[8,16]{1,0:T(8,128)S(1)} %get-tuple-element.240.plan_ref, f32[8,32,8,128]{3,2,1,0:T(8,128)} %get-tuple-element.241.patches_ref), custom_call_target="tpu_custom_call" | custom-call | flops 16777216 | bytes 2097152 | tf_op jit(solution)/shard_map/cond/branch_5_fun/settle/pallas_call | solution.py:331
  16.1 6.1 %collective-permute-done.15.refs_0_ = f32[33,8,128]{2,1,0:T(8,128)S(1)} collective-permute-done((f32[33,8,128]{2,1,0:T(8,128)S(1)}, f32[33,8,128]{2,1,0:T(8,128)S(1)}, u32[]{:S(2)}, u32[]{:S(2)}) %collective-permute-start.15) | collective-permute-done | bytes 135200 | tf_op jit(solution)/shard_map/cond/branch_5_fun/ppermute | solution.py:159
  22.2 0.4 %collective-permute-done.16.refs_1_ = f32[65,8,128]{2,1,0:T(8,128)S(1)} collective-permute-done((f32[65,8,128]{2,1,0:T(8,128)S(1)}, f32[65,8,128]{2,1,0:T(8,128)S(1)}, u32[]{:S(2)}, u32[]{:S(2)}) %collective-permute-start.16) | collective-permute-done | bytes 266272 | tf_op jit(solution)/shard_map/cond/branch_5_fun/ppermute | solution.py:159
  22.6 0.0 collective-permute-done.17.refs_2_
  22.6 1.6 %assemble.55 = (f32[8,32,8,128]{3,2,1,0:T(8,128)S(1)}, f32[3,8,128]{2,1,0:T(8,128)S(1)}) custom-call(s32[8,16]{1,0:T(8,128)S(1)} %get-tuple-element.240.plan_ref, f32[8,32,8,128]{3,2,1,0:T(8,128)} %get-tuple-element.241.patches_ref, f32[33,8,128]{2,1,0:T(8,128)S(1)} %collective-permute-done.15.refs_0_, f32[65,8,128]{2,1,0:T(8,128)S(1)} %collective-permute-done.16.refs_1_, ...), custom_call_target="tpu_custom_call" | custom-call | tf_op jit(solution)/shard_map/cond/branch_5_fun/assemble/pallas_call | solution.py:387
  24.4 1.4 %collective-permute-start.154 = (f32[8,128]{1,0:T(8,128)S(1)}, f32[8,128]{1,0:T(8,128)S(1)}, u32[]{:S(2)}, u32[]{:S(2)}) collective-permute-start(f32[8,128]{1,0:T(8,128)S(1)} %get-tuple-element.565), channel_id=1, source_target_pairs={{4,3},{8,7},{12,11},{16,15},{20,19},{24,23},{28,27}} | collective-permute-start | bytes 12296 | tf_op jit(solution)/shard_map/ppermute | solution.py:428
  25.8 4.0 %collective-permute-start.153 = (f32[8,128]{1,0:T(8,128)S(1)}, f32[8,128]{1,0:T(8,128)S(1)}, u32[]{:S(2)}, u32[]{:S(2)}) collective-permute-start(f32[8,128]{1,0:T(8,128)S(1)} %get-tuple-element.566), channel_id=1, source_target_pairs={{0,4},{4,8},{8,12},{12,16},{16,20},{20,24},{24,28}} | collective-permute-start | bytes 12296 | tf_op jit(solution)/shard_map/ppermute | solution.py:426
  29.8 0.0 collective-permute-done.154.after_ref
  29.9 4.0 %collective-permute-done.153.before_ref = f32[8,128]{1,0:T(8,128)S(1)} collective-permute-done((f32[8,128]{1,0:T(8,128)S(1)}, f32[8,128]{1,0:T(8,128)S(1)}, u32[]{:S(2)}, u32[]{:S(2)}) %collective-permute-start.153) | collective-permute-done | bytes 4128 | tf_op jit(solution)/shard_map/ppermute | solution.py:426
  33.8 0.0 copy-done
  33.9 0.0 copy-done.1
  33.9 4.5 %refine.1 = bf16[8,64,4096]{2,1,0:T(8,128)(2,1)} custom-call(s32[8,16]{1,0:T(8,128)S(1)} %get-tuple-element.560.plan_ref, s32[1,32]{1,0:T(1,128)S(1)} %copy-done.1, f32[8,32,8,128]{3,2,1,0:T(8,128)S(1)} %get-tuple-element.562.held_ref, f32[8,32,8,128]{3,2,1,0:T(8,128)S(1)} %get-tuple-element.563.work_ref, f32[3,8,128]{2,1,0:T(8,128)S(1)} %get-tuple-element.564.ends_ref, ...), custom_call_target="tpu_custom_call" | custom-call | tf_op jit(solution)/shard_map/refine/pallas_call | solution.py:124
  (3 shorter events, 0.0 us)
Async XLA Ops:
  1.4 4.5 %collective-permute-start.152 = (s32[1,128]{1,0:T(1,128)S(1)}, s32[1,128]{1,0:T(1,128)S(1)}, u32[]{:S(2)}, u32[]{:S(2)}) collective-permute-start(s32[1,128]{1,0:T(1,128)S(1)} %pad.4), channel_id=1, source_target_pairs={{0,3},{1,2},{2,1},{3,0},{4,7},{5,6},{6,5},{7,4},{8,11},{9,10},{10,... | collective-permute-start | bytes 1544 | tf_op jit(solution)/shard_map/ppermute | solution.py:140
  3.9 3.6 %collective-permute-start.151 = (s32[1,128]{1,0:T(1,128)S(1)}, s32[1,128]{1,0:T(1,128)S(1)}, u32[]{:S(2)}, u32[]{:S(2)}) collective-permute-start(s32[1,128]{1,0:T(1,128)S(1)} %pad.4), channel_id=1, source_target_pairs={{0,2},{1,3},{2,0},{3,1},{4,6},{5,7},{6,4},{7,5},{8,10},{9,11},{10,... | collective-permute-start | bytes 1544 | tf_op jit(solution)/shard_map/ppermute | solution.py:140
  4.4 3.6 %collective-permute-start.150 = (s32[1,128]{1,0:T(1,128)S(1)}, s32[1,128]{1,0:T(1,128)S(1)}, u32[]{:S(2)}, u32[]{:S(2)}) collective-permute-start(s32[1,128]{1,0:T(1,128)S(1)} %pad.4), channel_id=1, source_target_pairs={{0,1},{1,0},{2,3},{3,2},{4,5},{5,4},{6,7},{7,6},{8,9},{9,8},{10,11... | collective-permute-start | bytes 1544 | tf_op jit(solution)/shard_map/ppermute | solution.py:140
  8.4 25.4 %copy-start = (bf16[256,256]{1,0:T(8,128)(2,1)S(1)}, bf16[256,256]{1,0:T(8,128)(2,1)}, u32[]{:S(2)}) copy-start(bf16[256,256]{1,0:T(8,128)(2,1)} %constant.17.clone.table_ref) | copy-start | bytes 393220
  8.4 25.4 %copy-start.1 = (s32[1,32]{1,0:T(1,128)S(1)}, s32[1,32]{1,0:T(1,128)}, u32[]{:S(2)}) copy-start(s32[1,32]{1,0:T(1,128)} %tag_ref.1) | copy-start | bytes 388
  10.4 12.2 %collective-permute-start.17 = (f32[66,8,128]{2,1,0:T(8,128)S(1)}, f32[66,8,128]{2,1,0:T(8,128)S(1)}, u32[]{:S(2)}, u32[]{:S(2)}) collective-permute-start(f32[66,8,128]{2,1,0:T(8,128)S(1)} %get-tuple-element.244), channel_id=1, source_target_pairs={{0,3},{1,0},{2,1},{3,2},{4,7},{5,4},{6,5},{7,6},{8,11},{9,8},{10,9... | collective-permute-start | bytes 811016 | tf_op jit(solution)/shard_map/cond/branch_5_fun/ppermute | solution.py:159
  11.9 10.7 %collective-permute-start.16 = (f32[65,8,128]{2,1,0:T(8,128)S(1)}, f32[65,8,128]{2,1,0:T(8,128)S(1)}, u32[]{:S(2)}, u32[]{:S(2)}) collective-permute-start(f32[65,8,128]{2,1,0:T(8,128)S(1)} %get-tuple-element.243), channel_id=1, source_target_pairs={{0,2},{1,3},{2,0},{3,1},{4,6},{5,7},{6,4},{7,5},{8,10},{9,11},{10,... | collective-permute-start | bytes 798728 | tf_op jit(solution)/shard_map/cond/branch_5_fun/ppermute | solution.py:159
  12.4 9.7 %collective-permute-start.15 = (f32[33,8,128]{2,1,0:T(8,128)S(1)}, f32[33,8,128]{2,1,0:T(8,128)S(1)}, u32[]{:S(2)}, u32[]{:S(2)}) collective-permute-start(f32[33,8,128]{2,1,0:T(8,128)S(1)} %get-tuple-element.242), channel_id=1, source_target_pairs={{0,1},{1,2},{2,3},{3,0},{4,5},{5,6},{6,7},{7,4},{8,9},{9,10},{10,1... | collective-permute-start | bytes 405512 | tf_op jit(solution)/shard_map/cond/branch_5_fun/ppermute | solution.py:159
  24.4 5.4 %collective-permute-start.154 = (f32[8,128]{1,0:T(8,128)S(1)}, f32[8,128]{1,0:T(8,128)S(1)}, u32[]{:S(2)}, u32[]{:S(2)}) collective-permute-start(f32[8,128]{1,0:T(8,128)S(1)} %get-tuple-element.565), channel_id=1, source_target_pairs={{4,3},{8,7},{12,11},{16,15},{20,19},{24,23},{28,27}} | collective-permute-start | bytes 12296 | tf_op jit(solution)/shard_map/ppermute | solution.py:428
  25.8 8.0 %collective-permute-start.153 = (f32[8,128]{1,0:T(8,128)S(1)}, f32[8,128]{1,0:T(8,128)S(1)}, u32[]{:S(2)}, u32[]{:S(2)}) collective-permute-start(f32[8,128]{1,0:T(8,128)S(1)} %get-tuple-element.566), channel_id=1, source_target_pairs={{0,4},{4,8},{8,12},{12,16},{16,20},{20,24},{24,28}} | collective-permute-start | bytes 12296 | tf_op jit(solution)/shard_map/ppermute | solution.py:426
